TPU v7x, 256 devices: a whole 4x4x8 slice. The times are simulated.
256 devices in a mesh: row: 16 (over y_hi, x, core), col: 16 (over z, y_lo).
Axes of the slice: x: 4, y: 4 (y_hi: 2, y_lo: 2; y = y_hi * 2 + y_lo), z: 8, core: 2. Of those that a mesh axis runs over, the one named last changes fastest.
Arguments:
- rho_real: float32 [8192, 8192], P('row', 'col'), may hold values from -6 to 12, as said below
- rho_imag: float32 [8192, 8192], P('row', 'col'), may hold values from -6 to 6, as said below
- gate_real_matrix: float32 [16, 16], replicated, may hold values from -1 to 1, as said below
- gate_imaginary: float32 [16, 16], replicated, may hold values from -1 to 1, as said below
- angles: float32 [8, 3], replicated, may hold values from -3.140625 to 3.140625
- targets: int32 [8], replicated, may hold values from 0 to 4
- gate_order: int32 [8], replicated, may hold values from 0 to 7, each once
Outputs:
- mixed_real: float32 [8192, 8192], P('row', 'col')
- depolarized_quadrature: float32 [8192, 8192], P('row', 'col')
- purity: float32 [], replicated
Inputs may be any that keep to these rules, and one draw needn't show every extreme that they name: rho_real is symmetric: entries of order one off the diagonal, each diagonal entry raised by 2 to 6. rho_imag is antisymmetric with a zero diagonal, so that rho_real + i rho_imag is Hermitian. gate_real_matrix + i gate_imaginary is a unitary matrix. gate_real_matrix + i gate_imaginary is a unitary matrix. `targets`: each gate acts on one of the 5 low qubits. `gate_order`: each gate appears once.
All inputs are finite; a program needn't handle non-finite values.
Results may differ from a plain program's by a relative error of at most 0.0001.
Values sent between devices are 32-bit elements; how exact they have to be, the bound alone decides.
A program may use at most 64 MiB of HBM per device.

v0:
```python
import functools

import jax
import jax.numpy as jnp
from jax import lax
from jax.experimental import pallas as pl
from jax.experimental.pallas import tpu as pltpu
from jax.sharding import PartitionSpec as P

MESH = pl.DeviceIdType.MESH
HIGHEST = lax.Precision.HIGHEST
MIX = 0.25
KEEP = 1 - MIX
GATE = 16
LOW = 32
GATES = 8
BLOCK = (2, 8, 128)


def ring(v):
    v %= 8
    return min(v, 8 - v)


STEPS = [4, 3, -3, 2, -2, 1, -1, 0]
UNITS = []
for beta_ in range(8):
    found = []
    for dz_ in STEPS:
        if ring(beta_ - dz_) >= ring(dz_):
            found.append((dz_, 0))
        if ring(beta_ - dz_) > ring(dz_):
            found.append((dz_, 1))
    UNITS.append(found)
BETAS = [7, 1, 6, 2, 5, 3, 4, 0]
FORWARDS = [(*UNITS[b_][u_], b_) for u_ in range(1, 8) for b_ in BETAS if UNITS[b_][u_][0] != 0]
SLOT = {f_: i_ for i_, f_ in enumerate(FORWARDS)}


def wrap(v, n):
    return jnp.where(v >= n, v - n, v)


def near(v):
    return jnp.minimum(v, 8 - v)


def pick(index, values):
    out = jnp.int32(values[0])
    for i, value in enumerate(values):
        if value != values[0]:
            out = jnp.where(index == i, value, out)
    return out


def lanes(shape=(8, 128)):
    return lax.broadcasted_iota(jnp.int32, shape, 1)


def exchange(t):
    lane = lanes()
    low = lane < 64
    even = (lane // 32) % 2 == 0
    u = [None] * 4
    for k in range(2):
        a, b = t[k], t[k + 2]
        turned = pltpu.roll(jnp.where(low, b, a), 64, 1)
        u[k] = jnp.where(low, a, turned)
        u[k + 2] = jnp.where(low, turned, b)
    out = []
    for i in range(2):
        a, b = u[2 * i], u[2 * i + 1]
        out.append(jnp.where(even, a, pltpu.roll(b, 32, 1)))
        out.append(jnp.where(even, pltpu.roll(a, 96, 1), b))
    return out


def pack(src, dst):
    def row(h, _):
        for part in range(2):
            for q in range(4):
                tiles = [
                    src[part, pl.ds(pl.multiple_of(32 * h + 8 * k, 8), 8), pl.ds(128 * q, 128)]
                    for k in range(4)
                ]
                for i, tile in enumerate(exchange(tiles)):
                    dst[16 * h + 4 * q + i, part] = tile
        return 0

    lax.fori_loop(0, 16, row, 0)


def exchange_kernel(
    re_ref, im_ref, f_ref, sums_ref, own, turned, pd, pe, mu, md, me, part_sums, plane_sums, load_sem, s1, ru, r1, r1z, s2, r2, sa, ra, sb, rb
):
    r, c = lax.axis_index("row"), lax.axis_index("col")
    z, ylo = c // 2, c % 2
    rho, core = r // 2, r % 2
    x, y = rho % 4, (rho // 4) * 2 + ylo
    partner = r + 1 - 2 * core
    beta = wrap(rho + 8 - z, 8)
    xs = [wrap(x + jx, 4) for jx in range(4)]
    xb = [wrap(x + 4 - jx, 4) for jx in range(4)]
    cores = (core, 1 - core)

    def plane(fn, lo, inner):
        def step(jy, _):
            yy = wrap(y + jy, 4)
            top = yy >= 2
            yh = jnp.where(top, 8, 0)
            p = jnp.where(top, yy - 2, yy)
            for jx, jc in inner:
                fn(yh + xs[jx] * 2 + cores[jc], p, jy * 8 + jx * 2 + jc)
            return 0

        lax.fori_loop(lo, 4, step, 0)

    def others(fn):
        plane(fn, 0, [(jx, jc) for jx in (1, 2, 3) for jc in (0, 1)])
        plane(fn, 1, [(0, 0), (0, 1)])

    def copy(src, dst, send, recv, row, col):
        return pltpu.make_async_remote_copy(src, dst, send, recv, device_id=(row, col), device_id_type=MESH)

    barrier = pltpu.get_barrier_semaphore()

    def greet(h, p, j):
        pl.semaphore_signal(barrier, inc=1, device_id=(h, 2 * z + p), device_id_type=MESH)

    others(greet)
    greet(partner, ylo, 0)
    for k in range(1, 8):
        for h in (r, partner):
            pl.semaphore_signal(barrier, inc=1, device_id=(h, 2 * wrap(z + k, 8) + ylo), device_id_type=MESH)

    loads = [
        pltpu.make_async_copy(ref.at[pl.ds(128 * i, 128)], own.at[part, pl.ds(128 * i, 128)], load_sem.at[part, i])
        for i in range(4)
        for part, ref in ((0, re_ref), (1, im_ref))
    ]
    for load in loads:
        load.start()
    for load in loads:
        load.wait()
    pack(own, pd)

    def turn(i, _):
        rows = pl.ds(pl.multiple_of(128 * i, 128), 128)
        for j in range(4):
            there = pl.ds(128 * j, 128)
            turned[0, there, rows] = own[0, rows, there].T
            turned[1, there, rows] = -own[1, rows, there].T
        return 0

    lax.fori_loop(0, 4, turn, 0)
    pack(turned, pe)
    packed = (pd, pe)

    pl.semaphore_wait(barrier, 45)

    def at_step(dz):
        zz = wrap(z + dz % 8, 8)
        b = wrap(rho + 8 - zz, 8)
        return zz, b, near(b) >= ring(dz), near(b) > ring(dz)

    def final(kind, b, co, dz, yl):
        a = (-dz) % 8
        return f_ref.at[2 * b + co, 2 * a + yl] if kind == 0 else f_ref.at[2 * a + yl, 2 * b + co]

    first = pick(beta, [UNITS[b][0][0] % 8 for b in range(8)])
    zf = wrap(z + first, 8)
    others(lambda h, p, j: copy(pd.at[16 * h + 2 * zf + p], mu.at[j], s1, ru.at[j], h, 2 * z + p).start())
    for dz in STEPS[:-1]:
        zz, b, direct, also = at_step(dz)
        for kind, valid in ((0, direct), (1, also)):
            if kind == 1 and ring(dz) == 4:
                continue

            @pl.when(valid)
            def _():
                for h in (r, partner):
                    copy(packed[kind].at[16 * h + 2 * zz + ylo], final(kind, b, core, dz, ylo), s2, r2, h, 2 * zz + ylo).start()

    for i, dz in enumerate(STEPS):
        zz, b, direct, also = at_step(dz)
        for kind, valid in ((0, direct), (1, also)):
            if dz == 0:
                dst, sem = final(kind, b, core, 0, ylo), r1z
            else:
                if not any(f[:2] == (dz, kind) for f in FORWARDS):
                    continue
                dst = md.at[i, 2 * b + core, ylo] if kind == 0 else me.at[i, ylo, 2 * b + core]
                sem = r1.at[pick(beta, [SLOT.get((dz, kind, bb), 0) for bb in range(8)])]
                if kind == 0:
                    valid = valid & (first != dz % 8)

            @pl.when(valid)
            def _():
                def send(h, p, j):
                    copy(packed[kind].at[16 * h + 2 * zz + p], dst, s1, sem, h, 2 * z + p).start()

                others(send)
                if dz == 0:
                    send(partner, ylo, 0)
                    dst[...] = packed[kind][16 * r + 2 * zz + ylo]


    def arrived(sem, count):
        copy(pd.at[pl.ds(0, count)], pe.at[pl.ds(0, count)], sem, sem, r, c).wait_recv()

    def left(sem, count):
        copy(pd.at[pl.ds(0, count)], pe.at[pl.ds(0, count)], sem, sem, r, c).wait_send()

    def either(condition, wait, sem, counts):
        @pl.when(condition)
        def _():
            wait(sem, counts[0])

        @pl.when(jnp.logical_not(condition))
        def _():
            wait(sem, counts[1])

    acc = jnp.zeros((8, 128), jnp.float32)

    def squares(i, acc):
        for part in range(2):
            for q in range(4):
                v = own[part, pl.ds(pl.multiple_of(8 * i, 8), 8), pl.ds(128 * q, 128)]
                acc = acc + v * v
        return acc

    total = jnp.sum(lax.fori_loop(0, 64, squares, acc))
    on_diagonal = lanes((128, 128)) == lax.broadcasted_iota(jnp.int32, (128, 128), 0)
    traces = []
    for part in range(2):
        v = sum(own[part, pl.ds(128 * q, 128), pl.ds(128 * q, 128)] for q in range(4))
        traces.append(jnp.where(r == c, jnp.sum(jnp.where(on_diagonal, v, 0.0)), 0.0))
    lane = lanes((1, 128))
    place = (y * 4 + x) * 2 + core
    part_sums[place] = jnp.where(lane == 0, total, jnp.where(lane == 1, traces[0], jnp.where(lane == 2, traces[1], 0.0)))

    def share(h, p, j):
        copy(part_sums.at[place], part_sums.at[place], sa, ra, h, 2 * z + p).start()

    others(share)
    share(partner, ylo, 0)

    def pass_on(lo, inner):
        def step(jy, _):
            yy = wrap(y + 4 - jy, 4)
            top = yy >= 2
            yh = jnp.where(top, 4, 0)
            yl = jnp.where(top, yy - 2, yy)
            for jx, jc in inner:
                j = jy * 8 + jx * 2 + jc
                bs = wrap(wrap(yh + xb[jx] + 8 - z, 8), 8)
                dz = pick(bs, [UNITS[b][0][0] % 8 for b in range(8)])
                a, b = wrap(8 - dz, 8), wrap(bs + 8 - dz, 8)
                copy(pd.at[0], mu.at[j], s1, ru.at[j], r, c).wait_recv()
                copy(mu.at[j], f_ref.at[2 * b + cores[jc], 2 * a + yl], s2, r2, r, 2 * wrap(z + dz, 8) + ylo).start()
            return 0

        lax.fori_loop(lo, 4, step, 0)

    pass_on(0, [(jx, jc) for jx in (1, 2, 3) for jc in (0, 1)])
    pass_on(1, [(0, 0), (0, 1)])
    for n, (dz, kind, bb) in enumerate(FORWARDS):
        i = STEPS.index(dz)
        a, b = (-dz) % 8, (bb - dz) % 8
        mine = beta == bb

        def onward(yl, count):
            if kind == 0:
                src, dst = md.at[i, pl.ds(2 * b, 2), pl.ds(yl, count)], f_ref.at[pl.ds(2 * b, 2), pl.ds(2 * a + yl, count)]
            else:
                src, dst = me.at[i, pl.ds(yl, count), pl.ds(2 * b, 2)], f_ref.at[pl.ds(2 * a + yl, count), pl.ds(2 * b, 2)]
            copy(src, dst, s2, r2, r, 2 * wrap(z + dz % 8, 8) + ylo).start()

        @pl.when(mine)
        def _():
            arrived(r1.at[n], 2)
            onward(1 - ylo, 1)

        @pl.when(jnp.logical_not(mine))
        def _():
            arrived(r1.at[n], 4)
            onward(0, 2)

    copy(part_sums.at[pl.ds(0, 31)], part_sums.at[pl.ds(0, 31)], sa, ra, r, c).wait_recv()
    plane_sums[z] = jnp.sum(part_sums[...], axis=0)
    for k in range(1, 8):
        copy(plane_sums.at[z], plane_sums.at[z], sb, rb, r, 2 * wrap(z + k, 8) + ylo).start()

    either(beta == 0, arrived, r1z, (59, 58))
    either(beta == 0, left, s1, (241, 242))
    left(s2, 196)
    copy(plane_sums.at[pl.ds(0, 7)], plane_sums.at[pl.ds(0, 7)], sb, rb, r, c).wait()
    copy(part_sums.at[pl.ds(0, 31)], part_sums.at[pl.ds(0, 31)], sa, ra, r, c).wait_send()
    sums_ref[...] = jnp.sum(plane_sums[...], axis=0)
    arrived(r2, 196)


def exchange_call(re, im):
    f32 = jnp.float32
    dma = pltpu.SemaphoreType.DMA
    blocks = lambda *n: pltpu.VMEM(n + BLOCK, f32)
    return pl.pallas_call(
        exchange_kernel,
        name="exchange",
        out_shape=(jax.ShapeDtypeStruct((16, 16) + BLOCK, f32), jax.ShapeDtypeStruct((1, 128), f32)),
        in_specs=[pl.BlockSpec(memory_space=pl.ANY)] * 2,
        out_specs=(pl.BlockSpec(memory_space=pltpu.VMEM), pl.BlockSpec(memory_space=pltpu.VMEM)),
        scratch_shapes=[
            pltpu.VMEM((2, 512, 512), f32),
            pltpu.VMEM((2, 512, 512), f32),
            blocks(256),
            blocks(256),
            blocks(32),
            blocks(7, 16, 2),
            blocks(7, 2, 16),
            pltpu.VMEM((32, 1, 128), f32),
            pltpu.VMEM((8, 1, 128), f32),
            dma((2, 4)),
            dma,
            dma((32,)),
            dma((len(FORWARDS),)),
            dma,
            dma,
            dma,
            dma,
            dma,
            dma,
            dma,
        ],
        compiler_params=pltpu.CompilerParams(collective_id=0, has_side_effects=True, vmem_limit_bytes=40 * 2**20),
    )(re, im)


def iota2(n, m, dim):
    return lax.broadcasted_iota(jnp.int32, (n, m), dim)


def halves(v):
    hi = v.astype(jnp.bfloat16)
    return hi, (v - hi.astype(jnp.float32)).astype(jnp.bfloat16)


def dot(a, b):
    return jnp.dot(a, b, preferred_element_type=jnp.float32)


def dot3(a, b):
    return dot(a[0], b[0]) + dot(a[0], b[1]) + dot(a[1], b[0])


def local_gate(angles, targets, order):
    theta, alpha, beta = angles[:, 0:1], angles[:, 1:2], angles[:, 2:3]
    cos, sin = jnp.cos(theta / 2), jnp.sin(theta / 2)
    both = alpha + beta
    elements = (
        (cos, cos * 0.0),
        (-jnp.cos(beta) * sin, -jnp.sin(beta) * sin),
        (jnp.cos(alpha) * sin, jnp.sin(alpha) * sin),
        (jnp.cos(both) * cos, jnp.sin(both) * cos),
    )
    i, j = iota2(64, 64, 0), iota2(64, 64, 1)
    left, right = i % 32, j % 32
    same_part, lower = i // 32 == j // 32, i // 32 > j // 32
    gates = lax.broadcasted_iota(jnp.int32, (GATES, 1), 0)
    total = jnp.where(iota2(64, 32, 0) == iota2(64, 32, 1), 1.0, 0.0)
    for position in range(GATES):
        gate = order[position]
        bit = jnp.left_shift(jnp.int32(1), targets[gate])
        entry = [
            [jnp.sum(jnp.where(gates == gate, e, 0.0), axis=0, keepdims=True) for e in pair] for pair in elements
        ]
        left_high, right_high = (left & bit) > 0, (right & bit) > 0
        same_rest = ((left ^ right) | bit) == bit
        step = [
            jnp.where(
                same_rest,
                jnp.where(
                    left_high,
                    jnp.where(right_high, entry[3][part], entry[2][part]),
                    jnp.where(right_high, entry[1][part], entry[0][part]),
                ),
                0.0,
            )
            for part in range(2)
        ]
        step = jnp.where(same_part, step[0], jnp.where(lower, step[1], -step[1]))
        total = jnp.dot(step, total, precision=HIGHEST, preferred_element_type=jnp.float32)
    return total


def spread(rows, small, cols):
    out = []
    for half in halves(small):
        wide = dot(rows, half).astype(jnp.bfloat16)
        out.append(lax.dot_general(wide, cols, (((1,), (1,)), ((), ())), preferred_element_type=jnp.float32))
    return out


def embed(re, im, part_i, part_j, keep, sign):
    same, lower = part_i == part_j, part_i > part_j
    out = []
    for a, b in zip(re, im):
        b = jnp.where(lower, b, -b) * sign
        out.append(jnp.where(keep, jnp.where(same, a, b), 0.0).astype(jnp.bfloat16))
    return out


def one_hot(n, m, index):
    return jnp.where(index == iota2(n, m, 1), 1.0, 0.0).astype(jnp.bfloat16)


def rotate_kernel(f_ref, sums_ref, ure_ref, uim_ref, angles_ref, targets_ref, order_ref, re_ref, im_ref, purity_ref, f1, f2, nat):
    r, c = lax.axis_index("row"), lax.axis_index("col")
    z = c // 2
    i, j = iota2(256, 256, 0), iota2(256, 256, 1)
    out_g = one_hot(256, 16, iota2(256, 16, 0) // 16)
    in_g = one_hot(256, 16, (iota2(256, 16, 0) // 16 + 2 * z) % 16)
    u_re, u_im = (spread(out_g, ref[...], in_g) for ref in (ure_ref, uim_ref))
    part_i, part_j, keep = (i // 8) % 2, (j // 8) % 2, i % 8 == j % 8
    u_left = embed(u_re, u_im, part_i, part_j, keep, 1.0)
    u_right = embed(u_re, u_im, part_i, part_j, keep, -1.0)
    gate = local_gate(angles_ref[...], targets_ref, order_ref)
    low = one_hot(256, 32, iota2(256, 32, 0) % 32)
    g_re, g_im = (spread(low, gate[32 * part : 32 * part + 32], low) for part in range(2))
    part_i, part_j, keep = i // 128, j // 128, (i // 32) % 4 == (j // 32) % 4
    g_left = embed(g_re, g_im, part_i, part_j, keep, 1.0)
    gt_re, gt_im = ([m.T for m in pair] for pair in (g_re, g_im))
    g_right = embed(gt_re, gt_im, part_i, part_j, keep, 1.0)

    def first(g, _):
        v = jnp.concatenate([f_ref[g, :, part].reshape(128, 128) for part in range(2)], axis=1)
        v = dot3(halves(v), g_right)
        for part in range(2):
            f1[g, :, part] = v[:, 128 * part : 128 * part + 128].reshape(16, 8, 128)
        return 0

    lax.fori_loop(0, 16, first, 0)

    def second(n, _):
        v = jnp.concatenate([f1[2 * n + k].reshape(256, 128) for k in range(2)], axis=1)
        v = dot3(u_right, halves(v))
        for k in range(2):
            f2[2 * n + k] = v[:, 128 * k : 128 * k + 128].reshape((16,) + BLOCK)
        return 0

    lax.fori_loop(0, 8, second, 0)

    def third(n, _):
        v = jnp.concatenate([f2[:, 2 * n + k].reshape(256, 128) for k in range(2)], axis=1)
        v = dot3(u_left, halves(v))
        for k in range(2):
            f1[:, 2 * n + k] = v[:, 128 * k : 128 * k + 128].reshape((16,) + BLOCK)
        return 0

    lax.fori_loop(0, 8, third, 0)

    def fourth(g, _):
        for part in range(2):
            for q in range(4):
                for k, tile in enumerate(exchange([f1[g, 4 * q + n, part] for n in range(4)])):
                    nat[part, pl.ds(pl.multiple_of(32 * g + 8 * k, 8), 8), pl.ds(128 * q, 128)] = tile
        return 0

    lax.fori_loop(0, 16, fourth, 0)

    sums = sums_ref[...]
    lane = lanes((1, 128))
    total, trace_re, trace_im = (jnp.sum(jnp.where(lane == n, sums, 0.0)) for n in range(3))
    dim = GATE * GATE * LOW
    shifts = (jnp.where(r == c, MIX * trace_re / dim, 0.0), jnp.where(r == c, MIX * trace_im / dim, 0.0))

    def fifth(n, _):
        rows = pl.ds(pl.multiple_of(128 * n, 128), 128)
        v = jnp.concatenate([nat[part, rows, :] for part in range(2)], axis=0)
        v = dot3(g_left, halves(v))
        diagonal = lax.broadcasted_iota(jnp.int32, (128, 512), 0) + 128 * n == lanes((128, 512))
        for part, ref in ((0, re_ref), (1, im_ref)):
            ref[rows, :] = KEEP * v[128 * part : 128 * part + 128] + jnp.where(diagonal, shifts[part], 0.0)
        return 0

    lax.fori_loop(0, 4, fifth, 0)
    squared = trace_re * trace_re + trace_im * trace_im
    purity_ref[0, 0] = (KEEP * KEEP * total + (2 * KEEP * MIX + MIX * MIX) * squared / dim) / (dim * dim)


def rotate_call(f, sums, u_re, u_im, angles, targets, order):
    f32 = jnp.float32
    vmem, smem = pl.BlockSpec(memory_space=pltpu.VMEM), pl.BlockSpec(memory_space=pltpu.SMEM)
    return pl.pallas_call(
        rotate_kernel,
        name="rotate",
        out_shape=(
            jax.ShapeDtypeStruct((512, 512), f32),
            jax.ShapeDtypeStruct((512, 512), f32),
            jax.ShapeDtypeStruct((1, 1), f32),
        ),
        in_specs=[vmem, vmem, vmem, vmem, vmem, smem, smem],
        out_specs=(vmem, vmem, smem),
        scratch_shapes=[
            pltpu.VMEM((16, 16) + BLOCK, f32),
            pltpu.VMEM((16, 16) + BLOCK, f32),
            pltpu.VMEM((2, 512, 512), f32),
        ],
        compiler_params=pltpu.CompilerParams(vmem_limit_bytes=40 * 2**20),
    )(f, sums, u_re, u_im, angles, targets, order)


def on_device(rho_real, rho_imag, gate_real_matrix, gate_imaginary, angles, targets, gate_order):
    f, sums = exchange_call(rho_real, rho_imag)
    re, im, purity = rotate_call(f, sums, gate_real_matrix, gate_imaginary, angles, targets, gate_order)
    return re, im, purity.reshape(())


def solution(mesh):
    return jax.shard_map(
        on_device,
        mesh=mesh,
        in_specs=(P("row", "col"), P("row", "col"), P(), P(), P(), P(), P()),
        out_specs=(P("row", "col"), P("row", "col"), P()),
        check_vma=False,
    )
```

profile of v0, /device:TPU:1, one launch (start us, length us, event | category | flops | bytes accessed | tf_op | source)
XLA Modules:
  0.0 72.7 jit_solution(16367188262682294516)
XLA Ops:
  0.6 0.0 copy-start.5
  0.6 0.0 copy-start.4
  0.7 0.8 %copy.10.angles_ref = f32[8,3]{1,0:T(8,128)S(1)} copy(f32[8,3]{0,1:T(4,128)} %param.11) | data formatting | bytes 192 | tf_op args[4]
  1.4 0.0 copy-start
  1.4 1.2 %copy-done = f32[512,512]{1,0:T(8,128)S(1)} copy-done((f32[512,512]{1,0:T(8,128)S(1)}, f32[512,512]{1,0:T(8,128)}, u32[]{:S(2)}) %copy-start) | copy-done | bytes 1048600
  2.6 0.0 copy-start.1
  2.6 1.2 %copy-done.1 = f32[512,512]{1,0:T(8,128)S(1)} copy-done((f32[512,512]{1,0:T(8,128)S(1)}, f32[512,512]{1,0:T(8,128)}, u32[]{:S(2)}) %copy-start.1) | copy-done | bytes 1048600
  3.9 0.0 copy-start.2
  3.9 0.0 copy-start.3
  3.9 51.9 %exchange.1 = (f32[16,16,2,8,128]{4,3,2,1,0:T(8,128)S(1)}, f32[1,128]{1,0:T(1,128)S(1)}) custom-call(f32[512,512]{1,0:T(8,128)S(1)} %copy-done, f32[512,512]{1,0:T(8,128)S(1)} %copy-done.1), custom_call_target="tpu_custom_call" | custom-call | tf_op jit(solution)/shard_map/exchange/pallas_call | solution.py:307
  55.8 0.0 copy-done.5
  55.8 0.0 copy-done.4
  55.8 0.0 copy-done.2
  55.8 0.0 copy-done.3
  55.8 16.9 %rotate.1 = (f32[512,512]{1,0:T(8,128)}, f32[512,512]{1,0:T(8,128)}, f32[1,1]{1,0:T(1,128)}) custom-call(f32[16,16,2,8,128]{4,3,2,1,0:T(8,128)S(1)} %get-tuple-element.8.f_ref, f32[1,128]{1,0:T(1,128)S(1)} %get-tuple-element.9.sums_ref, f32[16,16]{1,0:T(8,128)S(1)} %copy-done.2, f32[16,16]{1,0:T(8,128)S(1)} %copy-done.3, f32[8,3]{1,0:T(8,128)S(1)} %copy.10.angles_ref, ...), custom_call_target="tpu_custom_call" | custom-call | tf_op jit(solution)/shard_map/rotate/pallas_call | solution.py:494
Async XLA Ops:
  0.6 55.1 %copy-start.5 = (s32[8]{0:T(128)S(1)}, s32[8]{0:T(128)}, u32[]{:S(2)}) copy-start(s32[8]{0:T(128)} %order_ref.1) | copy-start | bytes 100
  0.6 55.1 %copy-start.4 = (s32[8]{0:T(128)S(1)}, s32[8]{0:T(128)}, u32[]{:S(2)}) copy-start(s32[8]{0:T(128)} %targets_ref.1) | copy-start | bytes 100
  1.4 1.2 %copy-start = (f32[512,512]{1,0:T(8,128)S(1)}, f32[512,512]{1,0:T(8,128)}, u32[]{:S(2)}) copy-start(f32[512,512]{1,0:T(8,128)} %re_ref.1) | copy-start | bytes 3145732
  2.6 1.2 %copy-start.1 = (f32[512,512]{1,0:T(8,128)S(1)}, f32[512,512]{1,0:T(8,128)}, u32[]{:S(2)}) copy-start(f32[512,512]{1,0:T(8,128)} %im_ref.1) | copy-start | bytes 3145732
  3.9 51.9 %copy-start.2 = (f32[16,16]{1,0:T(8,128)S(1)}, f32[16,16]{1,0:T(8,128)}, u32[]{:S(2)}) copy-start(f32[16,16]{1,0:T(8,128)} %ure_ref.1) | copy-start | bytes 3076
  3.9 51.9 %copy-start.3 = (f32[16,16]{1,0:T(8,128)S(1)}, f32[16,16]{1,0:T(8,128)}, u32[]{:S(2)}) copy-start(f32[16,16]{1,0:T(8,128)} %uim_ref.1) | copy-start | bytes 3076
where the time goes:
time: 72.9 us; the launch traced here: 72.7 us
  Pallas kernels  68.8 us (94%)
  local copies, waits for them, and re-layouts  3.23 us (4%)
    pallas_call x1, Pallas kernels, exchange_call(): pl.pallas_call(exchange_kernel, name='exchange', out_shape=(jax.ShapeDtyp...  51.9 us
    pallas_call x1, Pallas kernels, rotate_call(): pl.pallas_call(rotate_kernel, name='rotate', out_shape=(jax.ShapeDtypeStr...  16.9 us
    unnamed x13, local copies, waits for them, and re-layouts  3.23 us

commit v1 on v0

v1 whole, which is shorter than its diff:
```python
import functools

import jax
import jax.numpy as jnp
from jax import lax
from jax.experimental import pallas as pl
from jax.experimental.pallas import tpu as pltpu
from jax.sharding import PartitionSpec as P

MESH = pl.DeviceIdType.MESH
HIGHEST = lax.Precision.HIGHEST
MIX = 0.25
KEEP = 1 - MIX
GATE = 16
LOW = 32
GATES = 8
BLOCK = (2, 8, 128)


def ring(v):
    v %= 8
    return min(v, 8 - v)


STEPS = [4, 3, -3, 2, -2, 1, -1, 0]
UNITS = []
for beta_ in range(8):
    found = []
    for dz_ in STEPS:
        if ring(beta_ - dz_) >= ring(dz_):
            found.append((dz_, 0))
        if ring(beta_ - dz_) > ring(dz_):
            found.append((dz_, 1))
    UNITS.append(found)
BETAS = [7, 1, 6, 2, 5, 3, 4, 0]
FORWARDS = [(*UNITS[b_][u_], b_) for u_ in range(1, 8) for b_ in BETAS if UNITS[b_][u_][0] != 0]
GROUP = {dz_: int(ring(dz_) == 1) for dz_ in STEPS}
SLOT = {f_: i_ for i_, f_ in enumerate(FORWARDS)}


def wrap(v, n):
    return jnp.where(v >= n, v - n, v)


def near(v):
    return jnp.minimum(v, 8 - v)


def pick(index, values):
    out = jnp.int32(values[0])
    for i, value in enumerate(values):
        if value != values[0]:
            out = jnp.where(index == i, value, out)
    return out


def lanes(shape=(8, 128)):
    return lax.broadcasted_iota(jnp.int32, shape, 1)


def exchange(t):
    lane = lanes()
    low = lane < 64
    even = (lane // 32) % 2 == 0
    u = [None] * 4
    for k in range(2):
        a, b = t[k], t[k + 2]
        turned = pltpu.roll(jnp.where(low, b, a), 64, 1)
        u[k] = jnp.where(low, a, turned)
        u[k + 2] = jnp.where(low, turned, b)
    out = []
    for i in range(2):
        a, b = u[2 * i], u[2 * i + 1]
        out.append(jnp.where(even, a, pltpu.roll(b, 32, 1)))
        out.append(jnp.where(even, pltpu.roll(a, 96, 1), b))
    return out


def pack(src, dst, i):
    for n in range(4):
        h = 4 * i + n
        for part in range(2):
            for q in range(4):
                tiles = [
                    src[part, pl.ds(pl.multiple_of(32 * h + 8 * k, 8), 8), pl.ds(128 * q, 128)]
                    for k in range(4)
                ]
                for m, tile in enumerate(exchange(tiles)):
                    dst[16 * h + 4 * q + m, part] = tile


def exchange_kernel(
    re_hbm, im_hbm, ure_hbm, uim_hbm, angles_hbm, targets_hbm, order_hbm, out_ref, left_ref, sums_ref,
    own, turned, pd, pe, mu, md, me, f_ref, part_sums, plane_sums, small, angles, targets, order, right1, right2,
    load_sem, small_sem, s1, ru, r1, r1z, s2, r2, sa, ra, sb, rb,
):
    r, c = lax.axis_index("row"), lax.axis_index("col")
    z, ylo = c // 2, c % 2
    rho, core = r // 2, r % 2
    x, y = rho % 4, (rho // 4) * 2 + ylo
    partner = r + 1 - 2 * core
    beta = wrap(rho + 8 - z, 8)
    xs = [wrap(x + jx, 4) for jx in range(4)]
    xb = [wrap(x + 4 - jx, 4) for jx in range(4)]
    cores = (core, 1 - core)

    def plane(fn, lo, inner):
        def step(jy, _):
            yy = wrap(y + jy, 4)
            top = yy >= 2
            yh = jnp.where(top, 8, 0)
            p = jnp.where(top, yy - 2, yy)
            for jx, jc in inner:
                fn(yh + xs[jx] * 2 + cores[jc], p, jy * 8 + jx * 2 + jc)
            return 0

        lax.fori_loop(lo, 4, step, 0)

    def others(fn):
        plane(fn, 0, [(jx, jc) for jx in (1, 2, 3) for jc in (0, 1)])
        plane(fn, 1, [(0, 0), (0, 1)])

    def copy(src, dst, send, recv, row, col):
        return pltpu.make_async_remote_copy(src, dst, send, recv, device_id=(row, col), device_id_type=MESH)

    loads = [
        [
            pltpu.make_async_copy(ref.at[pl.ds(128 * i, 128)], own.at[part, pl.ds(128 * i, 128)], load_sem.at[part, i])
            for part, ref in ((0, re_hbm), (1, im_hbm))
        ]
        for i in range(4)
    ]
    for pair in loads:
        for load in pair:
            load.start()
    barrier = pltpu.get_barrier_semaphore()

    def greet(h, p, j):
        pl.semaphore_signal(barrier, inc=1, device_id=(h, 2 * z + p), device_id_type=MESH)

    others(greet)
    greet(partner, ylo, 0)
    for k in range(1, 8):
        for h in (r, partner):
            pl.semaphore_signal(barrier, inc=1, device_id=(h, 2 * wrap(z + k, 8) + ylo), device_id_type=MESH)
    smalls = [
        pltpu.make_async_copy(ref, dst, small_sem.at[i])
        for i, (ref, dst) in enumerate(
            (
                (ure_hbm, small.at[0]),
                (uim_hbm, small.at[1]),
                (angles_hbm, angles),
                (targets_hbm, targets),
                (order_hbm, order),
            )
        )
    ]
    for load in smalls:
        load.start()
    for i, pair in enumerate(loads):
        for load in pair:
            load.wait()
        pack(own, pd, i)
    packed = (pd, pe)
    pl.semaphore_wait(barrier, 45)

    def at_step(dz):
        zz = wrap(z + dz % 8, 8)
        b = wrap(rho + 8 - zz, 8)
        return zz, b, near(b) >= ring(dz), near(b) > ring(dz)

    def final(kind, b, co, dz, yl):
        a = (-dz) % 8
        return f_ref.at[2 * b + co, 2 * a + yl] if kind == 0 else f_ref.at[2 * a + yl, 2 * b + co]

    first = pick(beta, [UNITS[b][0][0] % 8 for b in range(8)])
    zf = wrap(z + first, 8)
    others(lambda h, p, j: copy(pd.at[16 * h + 2 * zf + p], mu.at[j], s1, ru.at[j], h, 2 * z + p).start())
    def straight(kind):
        for dz in STEPS[:-1]:
            zz, b, direct, also = at_step(dz)
            if kind == 1 and ring(dz) == 4:
                continue

            @pl.when(also if kind else direct)
            def _():
                for h in (r, partner):
                    copy(
                        packed[kind].at[16 * h + 2 * zz + ylo],
                        final(kind, b, core, dz, ylo),
                        s2,
                        r2.at[GROUP[dz]],
                        h,
                        2 * zz + ylo,
                    ).start()

    def send_units(steps):
        for dz in steps:
            i = STEPS.index(dz)
            zz, b, direct, also = at_step(dz)
            for kind, valid in ((0, direct), (1, also)):
                if dz == 0:
                    dst, sem = final(kind, b, core, 0, ylo), r1z
                else:
                    if not any(f[:2] == (dz, kind) for f in FORWARDS):
                        continue
                    dst = md.at[i, 2 * b + core, ylo] if kind == 0 else me.at[i, ylo, 2 * b + core]
                    sem = r1.at[pick(beta, [SLOT.get((dz, kind, bb), 0) for bb in range(8)])]
                    if kind == 0:
                        valid = valid & (first != dz % 8)

                @pl.when(valid)
                def _():
                    def send(h, p, j):
                        copy(packed[kind].at[16 * h + 2 * zz + p], dst, s1, sem, h, 2 * z + p).start()

                    others(send)
                    if dz == 0:
                        send(partner, ylo, 0)
                        dst[...] = packed[kind][16 * r + 2 * zz + ylo]

    straight(0)
    for i in range(4):
        rows = pl.ds(128 * i, 128)
        for j in range(4):
            there = pl.ds(128 * j, 128)
            turned[0, there, rows] = own[0, rows, there].T
            turned[1, there, rows] = -own[1, rows, there].T

    for i in range(4):
        pack(turned, pe, i)
    straight(1)
    send_units(STEPS[:5])

    def arrived(sem, count):
        copy(pd.at[pl.ds(0, count)], pe.at[pl.ds(0, count)], sem, sem, r, c).wait_recv()

    def left(sem, count):
        copy(pd.at[pl.ds(0, count)], pe.at[pl.ds(0, count)], sem, sem, r, c).wait_send()

    def either(condition, wait, sem, counts):
        @pl.when(condition)
        def _():
            wait(sem, counts[0])

        @pl.when(jnp.logical_not(condition))
        def _():
            wait(sem, counts[1])

    def pass_on(lo, inner):
        def step(jy, _):
            yy = wrap(y + 4 - jy, 4)
            top = yy >= 2
            yh = jnp.where(top, 4, 0)
            yl = jnp.where(top, yy - 2, yy)
            for jx, jc in inner:
                j = jy * 8 + jx * 2 + jc
                bs = wrap(wrap(yh + xb[jx] + 8 - z, 8), 8)
                dz = pick(bs, [UNITS[b][0][0] % 8 for b in range(8)])
                a, b = wrap(8 - dz, 8), wrap(bs + 8 - dz, 8)
                copy(pd.at[0], mu.at[j], s1, ru.at[j], r, c).wait_recv()
                copy(mu.at[j], f_ref.at[2 * b + cores[jc], 2 * a + yl], s2, r2.at[0], r, 2 * wrap(z + dz, 8) + ylo).start()
            return 0

        lax.fori_loop(lo, 4, step, 0)

    pass_on(0, [(jx, jc) for jx in (1, 2, 3) for jc in (0, 1)])
    pass_on(1, [(0, 0), (0, 1)])
    send_units(STEPS[5:])

    acc = jnp.zeros((8, 128), jnp.float32)

    def squares(i, acc):
        for part in range(2):
            for q in range(4):
                v = own[part, pl.ds(pl.multiple_of(8 * i, 8), 8), pl.ds(128 * q, 128)]
                acc = acc + v * v
        return acc

    total = jnp.sum(lax.fori_loop(0, 64, squares, acc))
    on_diagonal = lanes((128, 128)) == lax.broadcasted_iota(jnp.int32, (128, 128), 0)
    traces = []
    for part in range(2):
        v = sum(own[part, pl.ds(128 * q, 128), pl.ds(128 * q, 128)] for q in range(4))
        traces.append(jnp.where(r == c, jnp.sum(jnp.where(on_diagonal, v, 0.0)), 0.0))
    lane = lanes((1, 128))
    place = (y * 4 + x) * 2 + core
    part_sums[place] = jnp.where(lane == 0, total, jnp.where(lane == 1, traces[0], jnp.where(lane == 2, traces[1], 0.0)))

    def share(h, p, j):
        copy(part_sums.at[place], part_sums.at[place], sa, ra, h, 2 * z + p).start()

    others(share)
    share(partner, ylo, 0)

    for n, (dz, kind, bb) in enumerate(FORWARDS):
        i = STEPS.index(dz)
        a, b = (-dz) % 8, (bb - dz) % 8
        mine = beta == bb

        def onward(yl, count):
            if kind == 0:
                src, dst = md.at[i, pl.ds(2 * b, 2), pl.ds(yl, count)], f_ref.at[pl.ds(2 * b, 2), pl.ds(2 * a + yl, count)]
            else:
                src, dst = me.at[i, pl.ds(yl, count), pl.ds(2 * b, 2)], f_ref.at[pl.ds(2 * a + yl, count), pl.ds(2 * b, 2)]
            copy(src, dst, s2, r2.at[GROUP[dz]], r, 2 * wrap(z + dz % 8, 8) + ylo).start()

        @pl.when(mine)
        def _():
            arrived(r1.at[n], 2)
            onward(1 - ylo, 1)

        @pl.when(jnp.logical_not(mine))
        def _():
            arrived(r1.at[n], 4)
            onward(0, 2)

    copy(part_sums.at[pl.ds(0, 31)], part_sums.at[pl.ds(0, 31)], sa, ra, r, c).wait_recv()
    plane_sums[z] = jnp.sum(part_sums[...], axis=0)
    for k in range(1, 8):
        copy(plane_sums.at[z], plane_sums.at[z], sb, rb, r, 2 * wrap(z + k, 8) + ylo).start()

    for load in smalls:
        load.wait()
    prepare(z, small, angles, targets, order, right1, right2, left_ref)
    either(beta == 0, arrived, r1z, (59, 58))
    on_lanes(f_ref, right1, 0, 2, 0, 16)
    on_lanes(f_ref, right1, 2, 14, 0, 2)
    arrived(r2.at[0], 100)
    for n in range(5):
        on_lanes(f_ref, right1, 4 + 2 * n, 2, 4, 10)
    either(beta == 0, left, s1, (241, 242))
    left(s2, 196)
    copy(plane_sums.at[pl.ds(0, 7)], plane_sums.at[pl.ds(0, 7)], sb, rb, r, c).wait()
    copy(part_sums.at[pl.ds(0, 31)], part_sums.at[pl.ds(0, 31)], sa, ra, r, c).wait_send()
    sums_ref[...] = jnp.sum(plane_sums[...], axis=0)
    arrived(r2.at[1], 96)
    on_lanes(f_ref, right1, 2, 2, 2, 14)
    on_lanes(f_ref, right1, 14, 2, 2, 14)
    on_lanes(f_ref, right1, 4, 10, 2, 2)
    on_lanes(f_ref, right1, 4, 10, 14, 2)
    matrix = (right2[0], right2[1])
    for n in range(8):
        v = jnp.concatenate([f_ref[2 * n + k].reshape(256, 128) for k in range(2)], axis=1)
        v = dot3(matrix, halves(v))
        for k in range(2):
            out_ref[2 * n + k] = v[:, 128 * k : 128 * k + 128].reshape((16,) + BLOCK)


def exchange_call(*args):
    f32, bf16 = jnp.float32, jnp.bfloat16
    dma = pltpu.SemaphoreType.DMA
    vmem, hbm = pl.BlockSpec(memory_space=pltpu.VMEM), pl.BlockSpec(memory_space=pltpu.HBM)
    blocks = lambda *n: pltpu.VMEM(n + BLOCK, f32)
    return pl.pallas_call(
        exchange_kernel,
        name="exchange",
        out_shape=(
            jax.ShapeDtypeStruct((16, 16) + BLOCK, f32),
            jax.ShapeDtypeStruct((2, 256, 256), bf16),
            jax.ShapeDtypeStruct((1, 128), f32),
        ),
        in_specs=[hbm] * 7,
        out_specs=(vmem, vmem, vmem),
        scratch_shapes=[
            pltpu.VMEM((2, 512, 512), f32),
            pltpu.VMEM((2, 512, 512), f32),
            blocks(256),
            blocks(256),
            blocks(32),
            blocks(7, 16, 2),
            blocks(7, 2, 16),
            blocks(16, 16),
            pltpu.VMEM((32, 1, 128), f32),
            pltpu.VMEM((8, 1, 128), f32),
            pltpu.VMEM((2, 16, 16), f32),
            pltpu.VMEM((3, 8), f32),
            pltpu.SMEM((8,), jnp.int32),
            pltpu.SMEM((8,), jnp.int32),
            pltpu.VMEM((2, 256, 256), bf16),
            pltpu.VMEM((2, 256, 256), bf16),
            dma((2, 4)),
            dma((5,)),
            dma,
            dma((32,)),
            dma((len(FORWARDS),)),
            dma,
            dma,
            dma((2,)),
            dma,
            dma,
            dma,
            dma,
        ],
        compiler_params=pltpu.CompilerParams(collective_id=0, has_side_effects=True, vmem_limit_bytes=40 * 2**20),
    )(*args)


def iota2(n, m, dim):
    return lax.broadcasted_iota(jnp.int32, (n, m), dim)


def halves(v):
    hi = v.astype(jnp.bfloat16)
    return hi, (v - hi.astype(jnp.float32)).astype(jnp.bfloat16)


def dot(a, b):
    return jnp.dot(a, b, preferred_element_type=jnp.float32)


def dot3(a, b):
    return dot(a[0], b[0]) + dot(a[0], b[1]) + dot(a[1], b[0])


def gate_factors(angles, targets, order):
    theta, alpha, beta = angles[0:1], angles[1:2], angles[2:3]
    cos, sin = jnp.cos(theta / 2), jnp.sin(theta / 2)
    both = alpha + beta
    elements = (
        (cos, cos * 0.0),
        (-jnp.cos(beta) * sin, -jnp.sin(beta) * sin),
        (jnp.cos(alpha) * sin, jnp.sin(alpha) * sin),
        (jnp.cos(both) * cos, jnp.sin(both) * cos),
    )
    i, j = iota2(32, 32, 0), iota2(32, 32, 1)
    left, right, high = i % 8, j % 8, i >= 16
    same_part, lower, same_factor = (i // 8) % 2 == (j // 8) % 2, i > j, i // 16 == j // 16
    gates = lax.broadcasted_iota(jnp.int32, (1, GATES), 1)
    total = jnp.where((iota2(32, 8, 0) % 16) == iota2(32, 8, 1), 1.0, 0.0)
    for position in range(GATES):
        gate = order[position]
        target = targets[gate]
        low_bit = jnp.where(target == 0, 1, jnp.where(target == 1, 2, jnp.where(target == 2, 4, 0)))
        high_bit = jnp.where(target == 3, 1, jnp.where(target == 4, 2, 0))
        bit = jnp.where(high, high_bit, low_bit)
        entry = [
            [jnp.sum(jnp.where(gates == gate, e, 0.0), axis=1, keepdims=True) for e in pair] for pair in elements
        ]
        left_high, right_high = (left & bit) > 0, (right & bit) > 0
        same_rest = ((left ^ right) | bit) == bit
        step = [
            jnp.where(
                left_high,
                jnp.where(right_high, entry[3][part], entry[2][part]),
                jnp.where(right_high, entry[1][part], entry[0][part]),
            )
            for part in range(2)
        ]
        step = [jnp.where(bit > 0, v, one) for v, one in zip(step, (1.0, 0.0))]
        step = jnp.where(same_part, step[0], jnp.where(lower, step[1], -step[1]))
        step = jnp.where(same_rest & same_factor, step, 0.0)
        total = jnp.dot(step, total, precision=HIGHEST, preferred_element_type=jnp.float32)
    return total


def one_hot(n, m, index):
    return jnp.where(index == iota2(n, m, 1), 1.0, 0.0)


def spread(rows, small, cols):
    wide = jnp.dot(rows, small, precision=HIGHEST, preferred_element_type=jnp.float32)
    return lax.dot_general(wide, cols, (((1,), (1,)), ((), ())), precision=HIGHEST, preferred_element_type=jnp.float32)


def times(a, b):
    return a[0] * b[0] - a[1] * b[1], a[0] * b[1] + a[1] * b[0]


def store_halves(ref, v):
    hi, lo = halves(v)
    ref[0] = hi
    ref[1] = lo


def prepare(z, small, angles, targets, order, right1, right2, left_ref):
    i, j = iota2(256, 256, 0), iota2(256, 256, 1)
    row = lambda n: iota2(256, n, 0)
    factors = gate_factors(angles[...], targets, order)
    low, high = ([factors[16 * w + 8 * part : 16 * w + 8 * part + 8] for part in range(2)] for w in range(2))
    out_g = one_hot(256, 16, row(16) // 16)
    in_g = one_hot(256, 16, (row(16) // 16 + 2 * z) % 16)
    u = [spread(out_g, small[part], in_g) for part in range(2)]
    same, lower = (i // 8) % 2 == (j // 8) % 2, (i // 8) % 2 > (j // 8) % 2
    value = jnp.where(same, u[0], jnp.where(lower, -u[1], u[1]))
    store_halves(right2, jnp.where(i % 8 == j % 8, value, 0.0))
    on_s = one_hot(256, 8, row(8) % 8)
    value = times(u, [spread(on_s, m, on_s) for m in low])
    store_halves(left_ref, jnp.where(same, value[0], jnp.where(lower, value[1], -value[1])))
    on_k = one_hot(256, 8, (row(8) // 32) % 4)
    on_top = one_hot(256, 8, (row(8) // 8) % 4)
    turn = lambda hot, m: spread(hot, m.T, hot)
    a = [turn(on_k, m) for m in high]
    b = times([turn(on_top, m) for m in high], [turn(on_s, m) for m in low])
    value = times(a, (b[0], -b[1]))
    same, lower = i // 128 == j // 128, i > j
    store_halves(right1, jnp.where(same, value[0], jnp.where(lower, -value[1], value[1])))


def on_lanes(f_ref, right1, g, n, g2, n2):
    here = (pl.ds(g, n), pl.ds(g2, n2))
    v = jnp.concatenate([f_ref[(*here, part)].reshape(n * n2 * 8, 128) for part in range(2)], axis=1)
    v = dot3(halves(v), (right1[0], right1[1]))
    for part in range(2):
        f_ref[(*here, part)] = v[:, 128 * part : 128 * part + 128].reshape(n, n2, 8, 128)


def rotate_kernel(f_ref, left_ref, sums_ref, re_ref, im_ref, purity_ref, stage, sem):
    r, c = lax.axis_index("row"), lax.axis_index("col")
    sums = sums_ref[...]
    lane = lanes((1, 128))
    total, trace_re, trace_im = (jnp.sum(jnp.where(lane == n, sums, 0.0)) for n in range(3))
    dim = GATE * GATE * LOW
    shifts = (jnp.where(r == c, MIX * trace_re / dim, 0.0), jnp.where(r == c, MIX * trace_im / dim, 0.0))
    squared = trace_re * trace_re + trace_im * trace_im
    purity_ref[0, 0] = (KEEP * KEEP * total + (2 * KEEP * MIX + MIX * MIX) * squared / dim) / (dim * dim)
    matrix = (left_ref[0], left_ref[1])
    sublane = lax.broadcasted_iota(jnp.int32, (8, 128), 0)
    copies = []
    for q in range(4):
        v = jnp.concatenate([f_ref[:, 4 * q + n].reshape(256, 128) for n in range(4)], axis=1)
        v = dot3(matrix, halves(v))
        for g in range(16):
            for part in range(2):
                row = 16 * g + 8 * part
                tiles = exchange([v[row : row + 8, 128 * n : 128 * n + 128] for n in range(4)])
                for k, tile in enumerate(tiles):
                    tile = KEEP * tile
                    if g // 4 == q:
                        tile = tile + jnp.where(lanes() == sublane + (32 * (g % 4) + 8 * k), shifts[part], 0.0)
                    stage[part, q, 32 * g + 8 * k : 32 * g + 8 * k + 8] = tile
        for part, ref in ((0, re_ref), (1, im_ref)):
            copies.append(pltpu.make_async_copy(stage.at[part, q], ref.at[:, pl.ds(128 * q, 128)], sem.at[part, q]))
            copies[-1].start()
    for copy in copies:
        copy.wait()


def rotate_call(f, left, sums):
    f32 = jnp.float32
    vmem, hbm = pl.BlockSpec(memory_space=pltpu.VMEM), pl.BlockSpec(memory_space=pltpu.HBM)
    return pl.pallas_call(
        rotate_kernel,
        name="rotate",
        out_shape=(
            jax.ShapeDtypeStruct((512, 512), f32),
            jax.ShapeDtypeStruct((512, 512), f32),
            jax.ShapeDtypeStruct((1, 1), f32),
        ),
        in_specs=[vmem, vmem, vmem],
        out_specs=(hbm, hbm, pl.BlockSpec(memory_space=pltpu.SMEM)),
        scratch_shapes=[pltpu.VMEM((2, 4, 512, 128), f32), pltpu.SemaphoreType.DMA((2, 4))],
        compiler_params=pltpu.CompilerParams(vmem_limit_bytes=20 * 2**20),
    )(f, left, sums)


def on_device(rho_real, rho_imag, gate_real_matrix, gate_imaginary, angles, targets, gate_order):
    args = (rho_real, rho_imag, gate_real_matrix, gate_imaginary, angles.T, targets, gate_order)
    f, left, sums = exchange_call(*(pltpu.with_memory_space_constraint(v, pltpu.HBM) for v in args))
    re, im, purity = rotate_call(f, left, sums)
    return re, im, purity.reshape(())


def solution(mesh):
    return jax.shard_map(
        on_device,
        mesh=mesh,
        in_specs=(P("row", "col"), P("row", "col"), P(), P(), P(), P(), P()),
        out_specs=(P("row", "col"), P("row", "col"), P()),
        check_vma=False,
    )
```

time: 72.9 us -> 58.7 us (0.81)
  Pallas kernels: 68.8 us -> 57.8 us
  local copies, waits for them, and re-layouts: 3.23 us -> 0 us
    pallas_call x1, Pallas kernels: 16.9 us -> 2.61 us  [rotate_call(): pl.pallas_call(rotate_kernel, name='rotate', out_shape=(jax.ShapeDtypeStr...]
    pallas_call x1, Pallas kernels: 51.9 us -> 55.2 us  [exchange_call(): pl.pallas_call(exchange_kernel, name='exchange', out_shape=(jax.ShapeDtyp...]
    unnamed x13 -> x0, local copies, waits for them, and re-layouts: 3.23 us -> none
where the time goes in v1:
time: 58.7 us; the launch traced here: 58.6 us
  Pallas kernels  57.8 us (98%)
  between operations  0.8 us (1%)
    pallas_call x1, Pallas kernels, exchange_call(): pl.pallas_call(exchange_kernel, name='exchange', out_shape=(jax.ShapeDtyp...  55.2 us
    pallas_call x1, Pallas kernels, rotate_call(): pl.pallas_call(rotate_kernel, name='rotate', out_shape=(jax.ShapeDtypeStr...  2.61 us

profile of v1, /device:TPU:1, one launch (start us, length us, event | category | flops | bytes accessed | tf_op | source)
XLA Modules:
  0.0 58.6 jit_solution(16143956439759672267)
XLA Ops:
  0.6 55.2 %exchange.1 = (f32[16,16,2,8,128]{4,3,2,1,0:T(8,128)S(1)}, bf16[2,256,256]{2,1,0:T(8,128)(2,1)S(1)}, f32[1,128]{1,0:T(1,128)S(1)}) custom-call(f32[512,512]{1,0:T(8,128)} %re_hbm.1, f32[512,512]{1,0:T(8,128)} %im_hbm.1, f32[16,16]{1,0:T(8,128)} %ure_hbm.1, f32[16,16]{1,0:T(8,128)} %uim_hbm.1, f32[3,8]{1,0:T(4,128)} %bitcast.2, s32[8]{0:T(128)} %targets_hbm.1, ...), custom_call_target="tpu_custom_call" | custom-call | tf_op jit(solution)/shard_map/exchange/pallas_call | solution.py:355
  55.8 2.6 %rotate.1 = (f32[512,512]{1,0:T(8,128)}, f32[512,512]{1,0:T(8,128)}, f32[1,1]{1,0:T(1,128)}) custom-call(f32[16,16,2,8,128]{4,3,2,1,0:T(8,128)S(1)} %get-tuple-element.9.f_ref, bf16[2,256,256]{2,1,0:T(8,128)(2,1)S(1)} %get-tuple-element.10.left_ref, f32[1,128]{1,0:T(1,128)S(1)} %get-tuple-element.11.sums_ref), custom_call_target="tpu_custom_call" | custom-call | tf_op jit(solution)/shard_map/rotate/pallas_call | solution.py:542

commit v2 on v1

v2 whole, which is shorter than its diff:
```python
import functools

import jax
import jax.numpy as jnp
from jax import lax
from jax.experimental import pallas as pl
from jax.experimental.pallas import tpu as pltpu
from jax.sharding import PartitionSpec as P

MESH = pl.DeviceIdType.MESH
HIGHEST = lax.Precision.HIGHEST
MIX = 0.25
KEEP = 1 - MIX
GATE = 16
LOW = 32
GATES = 8
BLOCK = (2, 8, 128)


def ring(v):
    v %= 8
    return min(v, 8 - v)


STEPS = [4, 3, -3, 2, -2, 1, -1, 0]
UNITS = []
for beta_ in range(8):
    found = []
    for dz_ in STEPS:
        if ring(beta_ - dz_) >= ring(dz_):
            found.append((dz_, 0))
        if ring(beta_ - dz_) > ring(dz_):
            found.append((dz_, 1))
    UNITS.append(found)
CHIPS = sorted(((jx, jy) for jx in range(4) for jy in range(4) if jx or jy), key=lambda j: (min(j[0], 4 - j[0]) + min(j[1], 4 - j[1]), j))
OTHERS = [(jx, jy, jc) for jx, jy in CHIPS for jc in range(2)]
BETAS = [7, 1, 6, 2, 5, 3, 4, 0]
FORWARDS = [[(*UNITS[b_][u_], b_) for b_ in BETAS if UNITS[b_][u_][0] != 0] for u_ in range(8)]
SLOT = {f_: i_ for i_, f_ in enumerate(f_ for fs_ in FORWARDS[1:] for f_ in fs_)}
GROUP = {dz_: int(ring(dz_) == 1) for dz_ in STEPS}


def wrap(v, n):
    return jnp.where(v >= n, v - n, v)


def near(v):
    return jnp.minimum(v, 8 - v)


def pick(index, values):
    out = jnp.int32(values[0])
    for i, value in enumerate(values):
        if value != values[0]:
            out = jnp.where(index == i, value, out)
    return out


def lanes(shape=(8, 128)):
    return lax.broadcasted_iota(jnp.int32, shape, 1)


def halve(a, b, mask, shift):
    turned = pltpu.roll(jnp.where(mask, b, a), shift, 1)
    return jnp.where(mask, a, turned), jnp.where(mask, turned, b)


def pack(src, dst, tmp, i):
    low = lanes() < 64
    even = (lanes() // 32) % 2 == 0
    groups = [(4 * i + n, part, q) for n in range(4) for part in range(2) for q in range(4)]
    for n, (h, part, q) in enumerate(groups):
        tiles = [src[part, 32 * h + 8 * k : 32 * h + 8 * k + 8, 128 * q : 128 * q + 128] for k in range(4)]
        for k in range(2):
            tmp[n, k], tmp[n, k + 2] = halve(tiles[k], tiles[k + 2], low, 64)
    for n, (h, part, q) in enumerate(groups):
        for m in range(2):
            at = 16 * h + 4 * q + 2 * m
            dst[at, part], dst[at + 1, part] = halve(tmp[n, 2 * m], tmp[n, 2 * m + 1], even, 32)


def exchange_kernel(
    re_hbm, im_hbm, ure_hbm, uim_hbm, angles_hbm, targets_hbm, order_hbm, out_ref, left_ref, sums_ref,
    own, turned, packed, mu, passing, f_ref, part_sums, plane_sums, small, angles, targets, order, right1, right2, tmp,
    load_sem, small_sem, s1, ru, r1, r1z, s2, r2, sa, ra, sb, rb,
):
    r, c = lax.axis_index("row"), lax.axis_index("col")
    z, ylo = c // 2, c % 2
    rho, core = r // 2, r % 2
    x, y = rho % 4, (rho // 4) * 2 + ylo
    partner = r + 1 - 2 * core
    beta = wrap(rho + 8 - z, 8)
    cores = (core, 1 - core)
    ahead = [wrap(x + jx, 4) * 2 for jx in range(4)]
    behind = [wrap(x + 4 - jx, 4) for jx in range(4)]
    halves_of = lambda yy, top: (jnp.where(yy >= 2, top, 0), jnp.where(yy >= 2, yy - 2, yy))
    up = [halves_of(wrap(y + jy, 4), 8) for jy in range(4)]
    down = [halves_of(wrap(y + 4 - jy, 4), 4) for jy in range(4)]

    def others(fn):
        for j, (jx, jy, jc) in enumerate(OTHERS):
            fn(up[jy][0] + ahead[jx] + cores[jc], up[jy][1], j)

    def copy(src, dst, send, recv, row, col):
        return pltpu.make_async_remote_copy(src, dst, send, recv, device_id=(row, col), device_id_type=MESH)

    loads = [
        [
            pltpu.make_async_copy(ref.at[pl.ds(128 * i, 128)], own.at[part, pl.ds(128 * i, 128)], load_sem.at[part, i])
            for part, ref in ((0, re_hbm), (1, im_hbm))
        ]
        for i in range(4)
    ]
    barrier = pltpu.get_barrier_semaphore()
    for k in (4, 3, 5, 2, 6, 1, 7):
        for h in (r, partner):
            pl.semaphore_signal(barrier, inc=1, device_id=(h, 2 * wrap(z + k, 8) + ylo), device_id_type=MESH)
    for pair in loads:
        for load in pair:
            load.start()

    def greet(h, p, j):
        pl.semaphore_signal(barrier, inc=1, device_id=(h, 2 * z + p), device_id_type=MESH)

    others(greet)
    greet(partner, ylo, 0)
    smalls = [
        pltpu.make_async_copy(ref, dst, small_sem.at[i])
        for i, (ref, dst) in enumerate(
            (
                (ure_hbm, small.at[0]),
                (uim_hbm, small.at[1]),
                (angles_hbm, angles),
                (targets_hbm, targets),
                (order_hbm, order),
            )
        )
    ]
    for load in smalls:
        load.start()
    for i, pair in enumerate(loads):
        for load in pair:
            load.wait()
        pack(own, packed.at[0], tmp, i)
    for i in range(4):
        rows = pl.ds(128 * i, 128)
        for j in range(4):
            there = pl.ds(128 * j, 128)
            turned[0, there, rows] = own[0, rows, there].T
            turned[1, there, rows] = -own[1, rows, there].T

    pl.semaphore_wait(barrier, 45)

    def at_step(dz):
        zz = wrap(z + dz % 8, 8)
        b = wrap(rho + 8 - zz, 8)
        return zz, b, near(b) >= ring(dz), near(b) > ring(dz)

    def straight(kind):
        for dz in STEPS[:-1]:
            zz, b, direct, also = at_step(dz)
            if kind == 1 and ring(dz) == 4:
                continue
            a = (-dz) % 8

            @pl.when(also if kind else direct)
            def _():
                for h in (r, partner):
                    copy(
                        packed.at[kind, 16 * h + 2 * zz + ylo],
                        f_ref.at[2 * a + ylo, 2 * b + core] if kind else f_ref.at[2 * b + core, 2 * a + ylo],
                        s2,
                        r2.at[GROUP[dz]],
                        h,
                        2 * zz + ylo,
                    ).start()

    def send_unit(u):
        unit = [UNITS[b][u] for b in range(8)]
        dz = pick(beta, [d % 8 for d, _ in unit])
        kind = pick(beta, [k for _, k in unit])
        zz = wrap(z + dz, 8)
        b = wrap(beta + 8 - dz, 8)
        first, second = jnp.where(kind == 0, core, ylo), jnp.where(kind == 0, ylo, core)
        if u == 0:
            others(lambda h, p, j: copy(packed.at[0, 16 * h + 2 * zz + p], mu.at[j], s1, ru.at[j], h, 2 * z + p).start())
            return

        def passed():
            row = 112 * kind + 16 * pick(beta, [STEPS.index(d) % 7 for d, _ in unit]) + 2 * b + first
            sem = r1.at[pick(beta, [SLOT.get((*unit[bb], bb), 0) for bb in range(8)])]
            others(lambda h, p, j: copy(packed.at[kind, 16 * h + 2 * zz + p], passing.at[row, second], s1, sem, h, 2 * z + p).start())

        def kept():
            row, col = jnp.where(kind == 0, 2 * b + core, ylo), jnp.where(kind == 0, ylo, 2 * b + core)

            def send(h, p, j):
                copy(packed.at[kind, 16 * h + 2 * zz + p], f_ref.at[row, col], s1, r1z, h, 2 * z + p).start()

            others(send)
            send(partner, ylo, 0)
            f_ref[row, col] = packed[kind, 16 * r + 2 * zz + ylo]

        away = [d != 0 for d, _ in unit]
        if all(away):
            passed()
        elif not any(away):
            kept()
        else:
            pl.when(dz != 0)(passed)
            pl.when(dz == 0)(kept)

    send_unit(0)
    straight(0)
    for i in range(4):
        pack(turned, packed.at[1], tmp, i)
    straight(1)
    send_unit(1)

    def arrived(sem, count):
        copy(packed.at[0, pl.ds(0, count)], packed.at[1, pl.ds(0, count)], sem, sem, r, c).wait_recv()

    def left(sem, count):
        copy(packed.at[0, pl.ds(0, count)], packed.at[1, pl.ds(0, count)], sem, sem, r, c).wait_send()

    def either(condition, wait, sem, counts):
        @pl.when(condition)
        def _():
            wait(sem, counts[0])

        @pl.when(jnp.logical_not(condition))
        def _():
            wait(sem, counts[1])

    def share_sums():
        def squares(i, accs):
            for n in range(2):
                rows = pl.ds(pl.multiple_of(16 * i + 8 * n, 8), 8)
                tiles = [own[part, rows, pl.ds(128 * q, 128)] for part in range(2) for q in range(4)]
                accs = [acc + v * v for acc, v in zip(accs, tiles)]
            return accs

        total = jnp.sum(sum(lax.fori_loop(0, 32, squares, [jnp.zeros((8, 128), jnp.float32)] * 8)))
        on_diagonal = lanes((128, 128)) == lax.broadcasted_iota(jnp.int32, (128, 128), 0)
        traces = []
        for part in range(2):
            v = sum(own[part, pl.ds(128 * q, 128), pl.ds(128 * q, 128)] for q in range(4))
            traces.append(jnp.where(r == c, jnp.sum(jnp.where(on_diagonal, v, 0.0)), 0.0))
        lane = lanes((1, 128))
        place = (y * 4 + x) * 2 + core
        part_sums[place] = jnp.where(lane == 0, total, jnp.where(lane == 1, traces[0], jnp.where(lane == 2, traces[1], 0.0)))

        def share(h, p, j):
            copy(part_sums.at[place], part_sums.at[place], sa, ra, h, 2 * z + p).start()

        others(share)
        share(partner, ylo, 0)

    def pass_on():
        for j, (jx, jy, jc) in enumerate(OTHERS):
            bs = wrap(wrap(down[jy][0] + behind[jx] + 8 - z, 8), 8)
            dz = pick(bs, [UNITS[b][0][0] % 8 for b in range(8)])
            a, b = wrap(8 - dz, 8), wrap(bs + 8 - dz, 8)
            copy(mu.at[j], mu.at[j], s1, ru.at[j], r, c).wait_recv()
            dst = f_ref.at[2 * b + cores[jc], 2 * a + down[jy][1]]
            copy(mu.at[j], dst, s2, r2.at[0], r, 2 * wrap(z + dz, 8) + ylo).start()

    def forward(u):
        for dz, kind, bb in FORWARDS[u]:
            n = SLOT[dz, kind, bb]
            a, b = (-dz) % 8, (bb - dz) % 8
            row = 112 * kind + 16 * (STEPS.index(dz) % 7) + 2 * b
            mine = beta == bb

            def onward(full):
                if kind == 0:
                    first, second = (0, 2), (0, 2) if full else (1 - ylo, 1)
                else:
                    first, second = (0, 2) if full else (1 - ylo, 1), (0, 2)
                src = passing.at[pl.ds(row + first[0], first[1]), pl.ds(*second)]
                at = (2 * b, 2 * a) if kind == 0 else (2 * a, 2 * b)
                dst = f_ref.at[pl.ds(at[0] + first[0], first[1]), pl.ds(at[1] + second[0], second[1])]
                copy(src, dst, s2, r2.at[GROUP[dz]], r, 2 * wrap(z + dz % 8, 8) + ylo).start()

            @pl.when(mine)
            def _():
                arrived(r1.at[n], 2)
                onward(False)

            @pl.when(jnp.logical_not(mine))
            def _():
                arrived(r1.at[n], 4)
                onward(True)

    pass_on()
    for u in range(1, 7):
        send_unit(u + 1)
        if u == 3:
            share_sums()
        forward(u)

    copy(part_sums.at[pl.ds(0, 31)], part_sums.at[pl.ds(0, 31)], sa, ra, r, c).wait_recv()
    plane_sums[z] = jnp.sum(part_sums[...], axis=0)
    for k in range(1, 8):
        copy(plane_sums.at[z], plane_sums.at[z], sb, rb, r, 2 * wrap(z + k, 8) + ylo).start()

    for load in smalls:
        load.wait()
    prepare(z, ylo, small, angles, targets, order, right1, right2, left_ref)
    either(beta == 0, arrived, r1z, (59, 58))
    on_lanes(f_ref, right1, 0, 2, 0, 16)
    on_lanes(f_ref, right1, 2, 14, 0, 2)
    arrived(r2.at[0], 100)
    for n in range(5):
        on_lanes(f_ref, right1, 4 + 2 * n, 2, 4, 10)
    either(beta == 0, left, s1, (241, 242))
    left(s2, 196)
    copy(plane_sums.at[pl.ds(0, 7)], plane_sums.at[pl.ds(0, 7)], sb, rb, r, c).wait()
    copy(part_sums.at[pl.ds(0, 31)], part_sums.at[pl.ds(0, 31)], sa, ra, r, c).wait_send()
    sums_ref[...] = jnp.sum(plane_sums[...], axis=0)
    arrived(r2.at[1], 96)
    on_lanes(f_ref, right1, 2, 2, 2, 14)
    on_lanes(f_ref, right1, 14, 2, 2, 14)
    on_lanes(f_ref, right1, 4, 10, 2, 2)
    on_lanes(f_ref, right1, 4, 10, 14, 2)
    matrix = (right2[0], right2[1])
    for n in range(8):
        v = jnp.concatenate([f_ref[2 * n + k].reshape(256, 128) for k in range(2)], axis=1)
        v = dot3(matrix, halves(v))
        for k in range(2):
            out_ref[2 * n + k] = v[:, 128 * k : 128 * k + 128].reshape((16,) + BLOCK)


def exchange_call(*args):
    f32, bf16 = jnp.float32, jnp.bfloat16
    dma = pltpu.SemaphoreType.DMA
    vmem, hbm = pl.BlockSpec(memory_space=pltpu.VMEM), pl.BlockSpec(memory_space=pltpu.HBM)
    blocks = lambda *n: pltpu.VMEM(n + BLOCK, f32)
    return pl.pallas_call(
        exchange_kernel,
        name="exchange",
        out_shape=(
            jax.ShapeDtypeStruct((16, 16) + BLOCK, f32),
            jax.ShapeDtypeStruct((2, 256, 256), bf16),
            jax.ShapeDtypeStruct((1, 128), f32),
        ),
        in_specs=[hbm] * 7,
        out_specs=(vmem, vmem, vmem),
        scratch_shapes=[
            pltpu.VMEM((2, 512, 512), f32),
            pltpu.VMEM((2, 512, 512), f32),
            blocks(2, 256),
            blocks(32),
            blocks(224, 2),
            blocks(16, 16),
            pltpu.VMEM((32, 1, 128), f32),
            pltpu.VMEM((8, 1, 128), f32),
            pltpu.VMEM((2, 16, 16), f32),
            pltpu.VMEM((3, 8), f32),
            pltpu.SMEM((8,), jnp.int32),
            pltpu.SMEM((8,), jnp.int32),
            pltpu.VMEM((2, 256, 256), bf16),
            pltpu.VMEM((2, 256, 256), bf16),
            pltpu.VMEM((32, 4, 8, 128), f32),
            dma((2, 4)),
            dma((5,)),
            dma,
            dma((32,)),
            dma((len(SLOT),)),
            dma,
            dma,
            dma((2,)),
            dma,
            dma,
            dma,
            dma,
        ],
        compiler_params=pltpu.CompilerParams(collective_id=0, has_side_effects=True, vmem_limit_bytes=40 * 2**20),
    )(*args)


def iota2(n, m, dim):
    return lax.broadcasted_iota(jnp.int32, (n, m), dim)


def halves(v):
    hi = v.astype(jnp.bfloat16)
    return hi, (v - hi.astype(jnp.float32)).astype(jnp.bfloat16)


def dot(a, b):
    return jnp.dot(a, b, preferred_element_type=jnp.float32)


def dot3(a, b):
    return dot(a[0], b[0]) + dot(a[0], b[1]) + dot(a[1], b[0])


def gate_factors(angles, targets, order):
    theta, alpha, beta = angles[0:1], angles[1:2], angles[2:3]
    cos, sin = jnp.cos(theta / 2), jnp.sin(theta / 2)
    both = alpha + beta
    elements = (
        (cos, cos * 0.0),
        (-jnp.cos(beta) * sin, -jnp.sin(beta) * sin),
        (jnp.cos(alpha) * sin, jnp.sin(alpha) * sin),
        (jnp.cos(both) * cos, jnp.sin(both) * cos),
    )
    i, j = iota2(32, 32, 0), iota2(32, 32, 1)
    left, right, high = i % 8, j % 8, i >= 16
    same_part, lower, same_factor = (i // 8) % 2 == (j // 8) % 2, i > j, i // 16 == j // 16
    gates = lax.broadcasted_iota(jnp.int32, (1, GATES), 1)
    total = jnp.where((iota2(32, 8, 0) % 16) == iota2(32, 8, 1), 1.0, 0.0)
    for position in range(GATES):
        gate = order[position]
        target = targets[gate]
        low_bit = jnp.where(target == 0, 1, jnp.where(target == 1, 2, jnp.where(target == 2, 4, 0)))
        high_bit = jnp.where(target == 3, 1, jnp.where(target == 4, 2, 0))
        bit = jnp.where(high, high_bit, low_bit)
        entry = [
            [jnp.sum(jnp.where(gates == gate, e, 0.0), axis=1, keepdims=True) for e in pair] for pair in elements
        ]
        left_high, right_high = (left & bit) > 0, (right & bit) > 0
        same_rest = ((left ^ right) | bit) == bit
        step = [
            jnp.where(
                left_high,
                jnp.where(right_high, entry[3][part], entry[2][part]),
                jnp.where(right_high, entry[1][part], entry[0][part]),
            )
            for part in range(2)
        ]
        step = [jnp.where(bit > 0, v, one) for v, one in zip(step, (1.0, 0.0))]
        step = jnp.where(same_part, step[0], jnp.where(lower, step[1], -step[1]))
        step = jnp.where(same_rest & same_factor, step, 0.0)
        total = jnp.dot(step, total, precision=HIGHEST, preferred_element_type=jnp.float32)
    return total


def one_hot(n, m, index):
    return jnp.where(index == iota2(n, m, 1), 1.0, 0.0)


def spread(rows, small, cols):
    wide = jnp.dot(rows, small, precision=HIGHEST, preferred_element_type=jnp.float32)
    return lax.dot_general(wide, cols, (((1,), (1,)), ((), ())), precision=HIGHEST, preferred_element_type=jnp.float32)


def times(a, b):
    return a[0] * b[0] - a[1] * b[1], a[0] * b[1] + a[1] * b[0]


def store_halves(ref, v):
    hi, lo = halves(v)
    ref[0] = hi
    ref[1] = lo


def prepare(z, ylo, small, angles, targets, order, right1, right2, left_ref):
    i, j = iota2(256, 256, 0), iota2(256, 256, 1)
    row = lambda n: iota2(256, n, 0)
    factors = gate_factors(angles[...], targets, order)
    low, high = ([factors[16 * w + 8 * part : 16 * w + 8 * part + 8] for part in range(2)] for w in range(2))
    out_g = one_hot(256, 16, row(16) // 16)
    in_g = one_hot(256, 16, (row(16) // 16 + 2 * z) % 16)
    u = [spread(out_g, small[part], in_g) for part in range(2)]
    same, lower = (i // 8) % 2 == (j // 8) % 2, (i // 8) % 2 > (j // 8) % 2
    value = jnp.where(same, u[0], jnp.where(lower, -u[1], u[1]))
    store_halves(right2, jnp.where(i % 8 == j % 8, value, 0.0))
    on_s = one_hot(256, 8, row(8) % 8)
    value = times(u, [spread(on_s, m, on_s) for m in low])
    store_halves(left_ref, jnp.where(same, value[0], jnp.where(lower, value[1], -value[1])))
    k = (row(8) // 32) % 4
    on_k = one_hot(256, 8, k)
    from_k = one_hot(256, 8, jnp.where((ylo == 1) & (k % 2 == 0), 2 - k, k))
    on_top = one_hot(256, 8, (row(8) // 8) % 4)
    turn = lambda hot, m, to: spread(hot, m.T, to)
    a = [turn(from_k, m, on_k) for m in high]
    b = times([turn(on_top, m, on_top) for m in high], [turn(on_s, m, on_s) for m in low])
    value = times(a, (b[0], -b[1]))
    same, lower = i // 128 == j // 128, i > j
    store_halves(right1, jnp.where(same, value[0], jnp.where(lower, -value[1], value[1])))


def on_lanes(f_ref, right1, g, n, g2, n2):
    here = (pl.ds(g, n), pl.ds(g2, n2))
    v = jnp.concatenate([f_ref[(*here, part)].reshape(n * n2 * 8, 128) for part in range(2)], axis=1)
    v = dot3(halves(v), (right1[0], right1[1]))
    for part in range(2):
        f_ref[(*here, part)] = v[:, 128 * part : 128 * part + 128].reshape(n, n2, 8, 128)


def rotate_kernel(f_ref, left_ref, sums_ref, re_ref, im_ref, purity_ref, stage, tmp, sem):
    r, c = lax.axis_index("row"), lax.axis_index("col")
    sums = sums_ref[...]
    lane = lanes((1, 128))
    total, trace_re, trace_im = (jnp.sum(jnp.where(lane == n, sums, 0.0)) for n in range(3))
    dim = GATE * GATE * LOW
    shifts = (jnp.where(r == c, MIX * trace_re / dim, 0.0), jnp.where(r == c, MIX * trace_im / dim, 0.0))
    squared = trace_re * trace_re + trace_im * trace_im
    purity_ref[0, 0] = (KEEP * KEEP * total + (2 * KEEP * MIX + MIX * MIX) * squared / dim) / (dim * dim)
    matrix = (left_ref[0], left_ref[1])
    sublane = lax.broadcasted_iota(jnp.int32, (8, 128), 0)
    copies = []
    low = lanes() < 64
    even = (lanes() // 32) % 2 == 0
    for q in range(4):
        v = jnp.concatenate([f_ref[:, 4 * q + n].reshape(256, 128) for n in range(4)], axis=1)
        v = dot3(matrix, halves(v))
        for n in range(32):
            tiles = [v[8 * n : 8 * n + 8, 128 * m : 128 * m + 128] for m in range(4)]
            for m in range(2):
                tmp[n, m], tmp[n, m + 2] = halve(tiles[m], tiles[m + 2], low, 64)
        for n in range(32):
            g, part = n // 2, n % 2
            for m in range(2):
                a, b = KEEP * tmp[n, 2 * m], KEEP * tmp[n, 2 * m + 1]
                pair = (jnp.where(even, a, pltpu.roll(b, 32, 1)), jnp.where(even, pltpu.roll(a, 96, 1), b))
                for k, tile in zip((2 * m, 2 * m + 1), pair):
                    if g // 4 == q:
                        tile = tile + jnp.where(lanes() == sublane + (32 * (g % 4) + 8 * k), shifts[part], 0.0)
                    stage[part, q, 32 * g + 8 * k : 32 * g + 8 * k + 8] = tile
        for part, ref in ((0, re_ref), (1, im_ref)):
            copies.append(pltpu.make_async_copy(stage.at[part, q], ref.at[:, pl.ds(128 * q, 128)], sem.at[part, q]))
            copies[-1].start()
    for copy in copies:
        copy.wait()


def rotate_call(f, left, sums):
    f32 = jnp.float32
    vmem, hbm = pl.BlockSpec(memory_space=pltpu.VMEM), pl.BlockSpec(memory_space=pltpu.HBM)
    return pl.pallas_call(
        rotate_kernel,
        name="rotate",
        out_shape=(
            jax.ShapeDtypeStruct((512, 512), f32),
            jax.ShapeDtypeStruct((512, 512), f32),
            jax.ShapeDtypeStruct((1, 1), f32),
        ),
        in_specs=[vmem, vmem, vmem],
        out_specs=(hbm, hbm, pl.BlockSpec(memory_space=pltpu.SMEM)),
        scratch_shapes=[
            pltpu.VMEM((2, 4, 512, 128), f32),
            pltpu.VMEM((32, 4, 8, 128), f32),
            pltpu.SemaphoreType.DMA((2, 4)),
        ],
        compiler_params=pltpu.CompilerParams(vmem_limit_bytes=20 * 2**20),
    )(f, left, sums)


def on_device(rho_real, rho_imag, gate_real_matrix, gate_imaginary, angles, targets, gate_order):
    args = (rho_real, rho_imag, gate_real_matrix, gate_imaginary, angles.T, targets, gate_order)
    f, left, sums = exchange_call(*(pltpu.with_memory_space_constraint(v, pltpu.HBM) for v in args))
    re, im, purity = rotate_call(f, left, sums)
    return re, im, purity.reshape(())


def solution(mesh):
    return jax.shard_map(
        on_device,
        mesh=mesh,
        in_specs=(P("row", "col"), P("row", "col"), P(), P(), P(), P(), P()),
        out_specs=(P("row", "col"), P("row", "col"), P()),
        check_vma=False,
    )
```

time: 58.7 us -> 52.8 us (0.90)
  Pallas kernels: 57.8 us -> 51.9 us
    pallas_call x1, Pallas kernels: 55.2 us -> 49.2 us  [exchange_call(): pl.pallas_call(exchange_kernel, name='exchange', out_shape=(jax.ShapeDtyp...]
where the time goes in v2:
time: 52.8 us; the launch traced here: 52.7 us
  Pallas kernels  51.9 us (98%)
  between operations  0.8 us (2%)
    pallas_call x1, Pallas kernels, exchange_call(): pl.pallas_call(exchange_kernel, name='exchange', out_shape=(jax.ShapeDtyp...  49.2 us
    pallas_call x1, Pallas kernels, rotate_call(): pl.pallas_call(rotate_kernel, name='rotate', out_shape=(jax.ShapeDtypeStr...  2.64 us

profile of v2, /device:TPU:1, one launch (start us, length us, event | category | flops | bytes accessed | tf_op | source)
XLA Modules:
  0.0 52.7 jit_solution(2019870783046843964)
XLA Ops:
  0.6 49.2 %exchange.1 = (f32[16,16,2,8,128]{4,3,2,1,0:T(8,128)S(1)}, bf16[2,256,256]{2,1,0:T(8,128)(2,1)S(1)}, f32[1,128]{1,0:T(1,128)S(1)}) custom-call(f32[512,512]{1,0:T(8,128)} %re_hbm.1, f32[512,512]{1,0:T(8,128)} %im_hbm.1, f32[16,16]{1,0:T(8,128)} %ure_hbm.1, f32[16,16]{1,0:T(8,128)} %uim_hbm.1, f32[3,8]{1,0:T(4,128)} %bitcast.2, s32[8]{0:T(128)} %targets_hbm.1, ...), custom_call_target="tpu_custom_call" | custom-call | tf_op jit(solution)/shard_map/exchange/pallas_call | solution.py:339
  49.9 2.6 %rotate.1 = (f32[512,512]{1,0:T(8,128)}, f32[512,512]{1,0:T(8,128)}, f32[1,1]{1,0:T(1,128)}) custom-call(f32[16,16,2,8,128]{4,3,2,1,0:T(8,128)S(1)} %get-tuple-element.9.f_ref, bf16[2,256,256]{2,1,0:T(8,128)(2,1)S(1)} %get-tuple-element.10.left_ref, f32[1,128]{1,0:T(1,128)S(1)} %get-tuple-element.11.sums_ref), custom_call_target="tpu_custom_call" | custom-call | tf_op jit(solution)/shard_map/rotate/pallas_call | solution.py:533

commit v3 on v2

--- a/solution.py
+++ b/solution.py
@@ -23,21 +23,25 @@
 
 
 STEPS = [4, 3, -3, 2, -2, 1, -1, 0]
-UNITS = []
-for beta_ in range(8):
-    found = []
-    for dz_ in STEPS:
-        if ring(beta_ - dz_) >= ring(dz_):
-            found.append((dz_, 0))
-        if ring(beta_ - dz_) > ring(dz_):
-            found.append((dz_, 1))
-    UNITS.append(found)
+ORDER = [(d_, k_) for d_ in STEPS[:5] for k_ in (0, 1)] + [(d_, k_) for k_ in (0, 1) for d_ in (1, -1)] + [(0, 0), (0, 1)]
+UNITS = [
+    [(d_, k_) for d_, k_ in ORDER if ring(b_ - d_) >= ring(d_) + k_] for b_ in range(8)
+]
+BESIDE = {2: (1, 0), 3: (-1, 0)}
+UNITS[0] = [u_ for u_ in UNITS[0] if u_ not in BESIDE.values()] + [None, None]
 CHIPS = sorted(((jx, jy) for jx in range(4) for jy in range(4) if jx or jy), key=lambda j: (min(j[0], 4 - j[0]) + min(j[1], 4 - j[1]), j))
 OTHERS = [(jx, jy, jc) for jx, jy in CHIPS for jc in range(2)]
 BETAS = [7, 1, 6, 2, 5, 3, 4, 0]
-FORWARDS = [[(*UNITS[b_][u_], b_) for b_ in BETAS if UNITS[b_][u_][0] != 0] for u_ in range(8)]
+FORWARDS = [
+    [(*UNITS[b_][u_], b_) for b_ in BETAS if UNITS[b_][u_] and UNITS[b_][u_][0] != 0] + ([(*BESIDE[u_], 0)] if u_ in BESIDE else [])
+    for u_ in range(8)
+]
 SLOT = {f_: i_ for i_, f_ in enumerate(f_ for fs_ in FORWARDS[1:] for f_ in fs_)}
-GROUP = {dz_: int(ring(dz_) == 1) for dz_ in STEPS}
+AHEAD = {1:[2,3],2:[4],3:[5,6],4:[7],5:[]}
+
+
+def group(dz, kind):
+    return 1 + kind if ring(dz) == 1 else 0
 
 
 def wrap(v, n):
@@ -80,8 +84,8 @@
 
 
 def exchange_kernel(
-    re_hbm, im_hbm, ure_hbm, uim_hbm, angles_hbm, targets_hbm, order_hbm, out_ref, left_ref, sums_ref,
-    own, turned, packed, mu, passing, f_ref, part_sums, plane_sums, small, angles, targets, order, right1, right2, tmp,
+    re_hbm, im_hbm, ure_hbm, uim_hbm, angles_hbm, targets_hbm, order_hbm, early_ref, late_ref, matrix_ref, sums_ref,
+    own, turned, packed, mu, passing, f_ref, part_sums, plane_sums, small, angles, targets, order, factors, right1, right2, left, turned2, tmp,
     load_sem, small_sem, s1, ru, r1, r1z, s2, r2, sa, ra, sb, rb,
 ):
     r, c = lax.axis_index("row"), lax.axis_index("col")
@@ -170,13 +174,13 @@
                         packed.at[kind, 16 * h + 2 * zz + ylo],
                         f_ref.at[2 * a + ylo, 2 * b + core] if kind else f_ref.at[2 * b + core, 2 * a + ylo],
                         s2,
-                        r2.at[GROUP[dz]],
+                        r2.at[group(dz, kind)],
                         h,
                         2 * zz + ylo,
                     ).start()
 
     def send_unit(u):
-        unit = [UNITS[b][u] for b in range(8)]
+        unit = [UNITS[b][u] or (0, 0) for b in range(8)]
         dz = pick(beta, [d % 8 for d, _ in unit])
         kind = pick(beta, [k for _, k in unit])
         zz = wrap(z + dz, 8)
@@ -201,26 +205,37 @@
             send(partner, ylo, 0)
             f_ref[row, col] = packed[kind, 16 * r + 2 * zz + ylo]
 
-        away = [d != 0 for d, _ in unit]
-        if all(away):
-            passed()
-        elif not any(away):
-            kept()
-        else:
-            pl.when(dz != 0)(passed)
-            pl.when(dz == 0)(kept)
+        here = [UNITS[bb][u] is not None and UNITS[bb][u][0] == 0 for bb in range(8)]
+        away = [UNITS[bb][u] is not None and UNITS[bb][u][0] != 0 for bb in range(8)]
+        for which, action in ((away, passed), (here, kept)):
+            if all(which):
+                action()
+            elif any(which):
+                pl.when(pick(beta, [int(v) for v in which]) == 1)(action)
+
+        if u in BESIDE:
+
+            @pl.when(beta == 0)
+            def _():
+                d, k = BESIDE[u]
+                zb = wrap(z + d % 8, 8)
+                row = 112 * k + 16 * STEPS.index(d) + 2 * (-d % 8) + core
+                others(
+                    lambda h, p, j: copy(
+                        packed.at[k, 16 * h + 2 * zb + p], passing.at[row, ylo], s1, r1.at[SLOT[d, k, 0]], h, 2 * z + p
+                    ).start()
+                )
 
     send_unit(0)
     straight(0)
     for i in range(4):
         pack(turned, packed.at[1], tmp, i)
     straight(1)
-    send_unit(1)
 
     def arrived(sem, count):
         copy(packed.at[0, pl.ds(0, count)], packed.at[1, pl.ds(0, count)], sem, sem, r, c).wait_recv()
 
-    def left(sem, count):
+    def left_all(sem, count):
         copy(packed.at[0, pl.ds(0, count)], packed.at[1, pl.ds(0, count)], sem, sem, r, c).wait_send()
 
     def either(condition, wait, sem, counts):
@@ -258,6 +273,8 @@
 
     def pass_on():
         for j, (jx, jy, jc) in enumerate(OTHERS):
+            if j == 8:
+                send_unit(1)
             bs = wrap(wrap(down[jy][0] + behind[jx] + 8 - z, 8), 8)
             dz = pick(bs, [UNITS[b][0][0] % 8 for b in range(8)])
             a, b = wrap(8 - dz, 8), wrap(bs + 8 - dz, 8)
@@ -280,7 +297,7 @@
                 src = passing.at[pl.ds(row + first[0], first[1]), pl.ds(*second)]
                 at = (2 * b, 2 * a) if kind == 0 else (2 * a, 2 * b)
                 dst = f_ref.at[pl.ds(at[0] + first[0], first[1]), pl.ds(at[1] + second[0], second[1])]
-                copy(src, dst, s2, r2.at[GROUP[dz]], r, 2 * wrap(z + dz % 8, 8) + ylo).start()
+                copy(src, dst, s2, r2.at[group(dz, kind)], r, 2 * wrap(z + dz % 8, 8) + ylo).start()
 
             @pl.when(mine)
             def _():
@@ -293,10 +310,19 @@
                 onward(True)
 
     pass_on()
-    for u in range(1, 7):
-        send_unit(u + 1)
+    for load in smalls:
+        load.wait()
+    for u in range(1, 6):
+        for following in AHEAD[u]:
+            send_unit(following)
+        if u == 2:
+            factors[...] = gate_factors(angles[...], targets, order)
         if u == 3:
             share_sums()
+        if u == 4:
+            prepare_lanes(ylo, factors[...], right1)
+        if u == 5:
+            prepare_rows(z, factors[...], small, right2, left, matrix_ref)
         forward(u)
 
     copy(part_sums.at[pl.ds(0, 31)], part_sums.at[pl.ds(0, 31)], sa, ra, r, c).wait_recv()
@@ -304,31 +330,38 @@
     for k in range(1, 8):
         copy(plane_sums.at[z], plane_sums.at[z], sb, rb, r, 2 * wrap(z + k, 8) + ylo).start()
 
-    for load in smalls:
-        load.wait()
-    prepare(z, ylo, small, angles, targets, order, right1, right2, left_ref)
+    def over_g2(g, out):
+        v = jnp.concatenate([f_ref[g + n].reshape(256, 128) for n in range(2)], axis=1)
+        v = dot3((right2[0], right2[1]), halves(v))
+        for n in range(2):
+            out[n] = v[:, 128 * n : 128 * n + 128].reshape((16,) + BLOCK)
+
     either(beta == 0, arrived, r1z, (59, 58))
     on_lanes(f_ref, right1, 0, 2, 0, 16)
     on_lanes(f_ref, right1, 2, 14, 0, 2)
+    turned2[pl.ds(2, 2)] = jnp.zeros((2, 16) + BLOCK, jnp.float32)
+    turned2[pl.ds(14, 2)] = jnp.zeros((2, 16) + BLOCK, jnp.float32)
     arrived(r2.at[0], 100)
     for n in range(5):
         on_lanes(f_ref, right1, 4 + 2 * n, 2, 4, 10)
-    either(beta == 0, left, s1, (241, 242))
-    left(s2, 196)
+    arrived(r2.at[1], 56)
+    on_lanes(f_ref, right1, 2, 14, 2, 2)
+    on_lanes(f_ref, right1, 2, 14, 14, 2)
+    for g in (0, 4, 6, 8, 10, 12):
+        over_g2(g, turned2.at[pl.ds(g, 2)])
+    for n in range(8):
+        v = jnp.concatenate([turned2[:, 2 * n + m].reshape(256, 128) for m in range(2)], axis=1)
+        early_ref[n // 2, :, 256 * (n % 2) : 256 * (n % 2) + 256] = dot3((left[0], left[1]), halves(v))
+    either(beta == 0, left_all, s1, (241, 242))
+    left_all(s2, 196)
     copy(plane_sums.at[pl.ds(0, 7)], plane_sums.at[pl.ds(0, 7)], sb, rb, r, c).wait()
     copy(part_sums.at[pl.ds(0, 31)], part_sums.at[pl.ds(0, 31)], sa, ra, r, c).wait_send()
     sums_ref[...] = jnp.sum(plane_sums[...], axis=0)
-    arrived(r2.at[1], 96)
-    on_lanes(f_ref, right1, 2, 2, 2, 14)
-    on_lanes(f_ref, right1, 14, 2, 2, 14)
-    on_lanes(f_ref, right1, 4, 10, 2, 2)
-    on_lanes(f_ref, right1, 4, 10, 14, 2)
-    matrix = (right2[0], right2[1])
-    for n in range(8):
-        v = jnp.concatenate([f_ref[2 * n + k].reshape(256, 128) for k in range(2)], axis=1)
-        v = dot3(matrix, halves(v))
-        for k in range(2):
-            out_ref[2 * n + k] = v[:, 128 * k : 128 * k + 128].reshape((16,) + BLOCK)
+    arrived(r2.at[2], 40)
+    on_lanes(f_ref, right1, 2, 2, 4, 10)
+    on_lanes(f_ref, right1, 14, 2, 4, 10)
+    over_g2(2, late_ref.at[pl.ds(0, 2)])
+    over_g2(14, late_ref.at[pl.ds(2, 2)])
 
 
 def exchange_call(*args):
@@ -340,12 +373,13 @@
         exchange_kernel,
         name="exchange",
         out_shape=(
-            jax.ShapeDtypeStruct((16, 16) + BLOCK, f32),
-            jax.ShapeDtypeStruct((2, 256, 256), bf16),
+            jax.ShapeDtypeStruct((4, 256, 512), f32),
+            jax.ShapeDtypeStruct((4, 16) + BLOCK, f32),
+            jax.ShapeDtypeStruct((256, 256), bf16),
             jax.ShapeDtypeStruct((1, 128), f32),
         ),
         in_specs=[hbm] * 7,
-        out_specs=(vmem, vmem, vmem),
+        out_specs=(vmem, vmem, vmem, vmem),
         scratch_shapes=[
             pltpu.VMEM((2, 512, 512), f32),
             pltpu.VMEM((2, 512, 512), f32),
@@ -359,8 +393,11 @@
             pltpu.VMEM((3, 8), f32),
             pltpu.SMEM((8,), jnp.int32),
             pltpu.SMEM((8,), jnp.int32),
+            pltpu.VMEM((32, 8), f32),
             pltpu.VMEM((2, 256, 256), bf16),
             pltpu.VMEM((2, 256, 256), bf16),
+            pltpu.VMEM((2, 256, 256), bf16),
+            blocks(16, 16),
             pltpu.VMEM((32, 4, 8, 128), f32),
             dma((2, 4)),
             dma((5,)),
@@ -369,7 +406,7 @@
             dma((len(SLOT),)),
             dma,
             dma,
-            dma((2,)),
+            dma((3,)),
             dma,
             dma,
             dma,
@@ -456,24 +493,22 @@
     ref[1] = lo
 
 
-def prepare(z, ylo, small, angles, targets, order, right1, right2, left_ref):
+def of(factors, which):
+    return [factors[16 * which + 8 * part : 16 * which + 8 * part + 8] for part in range(2)]
+
+
+def by_row(n):
+    return iota2(256, n, 0)
+
+
+def prepare_lanes(ylo, factors, right1):
     i, j = iota2(256, 256, 0), iota2(256, 256, 1)
-    row = lambda n: iota2(256, n, 0)
-    factors = gate_factors(angles[...], targets, order)
-    low, high = ([factors[16 * w + 8 * part : 16 * w + 8 * part + 8] for part in range(2)] for w in range(2))
-    out_g = one_hot(256, 16, row(16) // 16)
-    in_g = one_hot(256, 16, (row(16) // 16 + 2 * z) % 16)
-    u = [spread(out_g, small[part], in_g) for part in range(2)]
-    same, lower = (i // 8) % 2 == (j // 8) % 2, (i // 8) % 2 > (j // 8) % 2
-    value = jnp.where(same, u[0], jnp.where(lower, -u[1], u[1]))
-    store_halves(right2, jnp.where(i % 8 == j % 8, value, 0.0))
-    on_s = one_hot(256, 8, row(8) % 8)
-    value = times(u, [spread(on_s, m, on_s) for m in low])
-    store_halves(left_ref, jnp.where(same, value[0], jnp.where(lower, value[1], -value[1])))
-    k = (row(8) // 32) % 4
+    low, high = of(factors, 0), of(factors, 1)
+    k = (by_row(8) // 32) % 4
     on_k = one_hot(256, 8, k)
     from_k = one_hot(256, 8, jnp.where((ylo == 1) & (k % 2 == 0), 2 - k, k))
-    on_top = one_hot(256, 8, (row(8) // 8) % 4)
+    on_top = one_hot(256, 8, (by_row(8) // 8) % 4)
+    on_s = one_hot(256, 8, by_row(8) % 8)
     turn = lambda hot, m, to: spread(hot, m.T, to)
     a = [turn(from_k, m, on_k) for m in high]
     b = times([turn(on_top, m, on_top) for m in high], [turn(on_s, m, on_s) for m in low])
@@ -482,6 +517,27 @@
     store_halves(right1, jnp.where(same, value[0], jnp.where(lower, -value[1], value[1])))
 
 
+def prepare_rows(z, factors, small, right2, left, late_ref):
+    i, j = iota2(256, 256, 0), iota2(256, 256, 1)
+    low = of(factors, 0)
+    out_g = one_hot(256, 16, by_row(16) // 16)
+    in_g = one_hot(256, 16, (by_row(16) // 16 + 2 * z) % 16)
+    u = [spread(out_g, small[part], in_g) for part in range(2)]
+    same, lower = (i // 8) % 2 == (j // 8) % 2, (i // 8) % 2 > (j // 8) % 2
+    value = jnp.where(same, u[0], jnp.where(lower, -u[1], u[1]))
+    store_halves(right2, jnp.where(i % 8 == j % 8, value, 0.0))
+    on_s = one_hot(256, 8, by_row(8) % 8)
+    low = [spread(on_s, m, on_s) for m in low]
+    real = lambda value: jnp.where(same, value[0], jnp.where(lower, value[1], -value[1]))
+    store_halves(left, real(times(u, low)))
+    n = (by_row(16) // 16) % 4
+    in_g = one_hot(256, 16, (n + jnp.where(n < 2, 2, 12) + 2 * z) % 16)
+    u = [spread(out_g, small[part], in_g) for part in range(2)]
+    hi, lo = (v.astype(jnp.float32) for v in halves(real(times(u, low))))
+    segment = j // 64
+    late_ref[...] = jnp.where(segment == 3, 0.0, jnp.where(segment == 1, lo, hi)).astype(jnp.bfloat16)
+
+
 def on_lanes(f_ref, right1, g, n, g2, n2):
     here = (pl.ds(g, n), pl.ds(g2, n2))
     v = jnp.concatenate([f_ref[(*here, part)].reshape(n * n2 * 8, 128) for part in range(2)], axis=1)
@@ -490,7 +546,7 @@
         f_ref[(*here, part)] = v[:, 128 * part : 128 * part + 128].reshape(n, n2, 8, 128)
 
 
-def rotate_kernel(f_ref, left_ref, sums_ref, re_ref, im_ref, purity_ref, stage, tmp, sem):
+def rotate_kernel(early_ref, late_ref, matrix_ref, sums_ref, re_ref, im_ref, purity_ref, stage, rotated, tmp, sem):
     r, c = lax.axis_index("row"), lax.axis_index("col")
     sums = sums_ref[...]
     lane = lanes((1, 128))
@@ -499,22 +555,29 @@
     shifts = (jnp.where(r == c, MIX * trace_re / dim, 0.0), jnp.where(r == c, MIX * trace_im / dim, 0.0))
     squared = trace_re * trace_re + trace_im * trace_im
     purity_ref[0, 0] = (KEEP * KEEP * total + (2 * KEEP * MIX + MIX * MIX) * squared / dim) / (dim * dim)
-    matrix = (left_ref[0], left_ref[1])
+    matrix = matrix_ref[...]
     sublane = lax.broadcasted_iota(jnp.int32, (8, 128), 0)
-    copies = []
     low = lanes() < 64
     even = (lanes() // 32) % 2 == 0
+    copies = []
+
+    def product(q):
+        v = jnp.concatenate([late_ref[:, 4 * q + m].reshape(64, 128) for m in range(4)], axis=1)
+        hi, lo = halves(v)
+        rotated[q] = early_ref[q] + dot(matrix, jnp.concatenate([hi, hi, lo, jnp.zeros_like(hi)], axis=0))
+
+    product(0)
     for q in range(4):
-        v = jnp.concatenate([f_ref[:, 4 * q + n].reshape(256, 128) for n in range(4)], axis=1)
-        v = dot3(matrix, halves(v))
+        if q < 3:
+            product(q + 1)
         for n in range(32):
-            tiles = [v[8 * n : 8 * n + 8, 128 * m : 128 * m + 128] for m in range(4)]
+            tiles = [rotated[q, 8 * n : 8 * n + 8, 128 * m : 128 * m + 128] for m in range(4)]
             for m in range(2):
-                tmp[n, m], tmp[n, m + 2] = halve(tiles[m], tiles[m + 2], low, 64)
+                tmp[q, n, m], tmp[q, n, m + 2] = halve(tiles[m], tiles[m + 2], low, 64)
         for n in range(32):
             g, part = n // 2, n % 2
             for m in range(2):
-                a, b = KEEP * tmp[n, 2 * m], KEEP * tmp[n, 2 * m + 1]
+                a, b = KEEP * tmp[q, n, 2 * m], KEEP * tmp[q, n, 2 * m + 1]
                 pair = (jnp.where(even, a, pltpu.roll(b, 32, 1)), jnp.where(even, pltpu.roll(a, 96, 1), b))
                 for k, tile in zip((2 * m, 2 * m + 1), pair):
                     if g // 4 == q:
@@ -527,7 +590,7 @@
         copy.wait()
 
 
-def rotate_call(f, left, sums):
+def rotate_call(*args):
     f32 = jnp.float32
     vmem, hbm = pl.BlockSpec(memory_space=pltpu.VMEM), pl.BlockSpec(memory_space=pltpu.HBM)
     return pl.pallas_call(
@@ -538,21 +601,22 @@
             jax.ShapeDtypeStruct((512, 512), f32),
             jax.ShapeDtypeStruct((1, 1), f32),
         ),
-        in_specs=[vmem, vmem, vmem],
+        in_specs=[vmem] * 4,
         out_specs=(hbm, hbm, pl.BlockSpec(memory_space=pltpu.SMEM)),
         scratch_shapes=[
             pltpu.VMEM((2, 4, 512, 128), f32),
-            pltpu.VMEM((32, 4, 8, 128), f32),
+            pltpu.VMEM((4, 256, 512), f32),
+            pltpu.VMEM((4, 32, 4, 8, 128), f32),
             pltpu.SemaphoreType.DMA((2, 4)),
         ],
         compiler_params=pltpu.CompilerParams(vmem_limit_bytes=20 * 2**20),
-    )(f, left, sums)
+    )(*args)
 
 
 def on_device(rho_real, rho_imag, gate_real_matrix, gate_imaginary, angles, targets, gate_order):
     args = (rho_real, rho_imag, gate_real_matrix, gate_imaginary, angles.T, targets, gate_order)
-    f, left, sums = exchange_call(*(pltpu.with_memory_space_constraint(v, pltpu.HBM) for v in args))
-    re, im, purity = rotate_call(f, left, sums)
+    found = exchange_call(*(pltpu.with_memory_space_constraint(v, pltpu.HBM) for v in args))
+    re, im, purity = rotate_call(*found)
     return re, im, purity.reshape(())
 
 

time: 52.8 us -> 51.1 us (0.968)
  Pallas kernels: 51.9 us -> 50.2 us
    pallas_call x1, Pallas kernels: 49.2 us -> 47.7 us  [exchange_call(): pl.pallas_call(exchange_kernel, name='exchange', out_shape=(jax.ShapeDtyp...]
where the time goes in v3:
time: 51.1 us; the launch traced here: 51 us
  Pallas kernels  50.2 us (98%)
  between operations  0.8 us (2%)
    pallas_call x1, Pallas kernels, exchange_call(): pl.pallas_call(exchange_kernel, name='exchange', out_shape=(jax.ShapeDtyp...  47.7 us
    pallas_call x1, Pallas kernels, rotate_call(): pl.pallas_call(rotate_kernel, name='rotate', out_shape=(jax.ShapeDtypeStr...  2.51 us

profile of v3, /device:TPU:1, one launch (start us, length us, event | category | flops | bytes accessed | tf_op | source)
XLA Modules:
  0.0 51.0 jit_solution(3339404615724719533)
XLA Ops:
  0.6 47.7 %exchange.1 = (f32[4,256,512]{2,1,0:T(8,128)S(1)}, f32[4,16,2,8,128]{4,3,2,1,0:T(8,128)S(1)}, bf16[256,256]{1,0:T(8,128)(2,1)S(1)}, f32[1,128]{1,0:T(1,128)S(1)}) custom-call(f32[512,512]{1,0:T(8,128)} %re_hbm.1, f32[512,512]{1,0:T(8,128)} %im_hbm.1, f32[16,16]{1,0:T(8,128)} %ure_hbm.1, f32[16,16]{1,0:T(8,128)} %uim_hbm.1, f32[3,8]{1,0:T(4,128)} %bitcast.2, ...), custom_call_target="tpu_custom_call" | custom-call | tf_op jit(solution)/shard_map/exchange/pallas_call | solution.py:372
  48.3 2.5 %rotate.1 = (f32[512,512]{1,0:T(8,128)}, f32[512,512]{1,0:T(8,128)}, f32[1,1]{1,0:T(1,128)}) custom-call(f32[4,256,512]{2,1,0:T(8,128)S(1)} %get-tuple-element.10.early_ref, f32[4,16,2,8,128]{4,3,2,1,0:T(8,128)S(1)} %get-tuple-element.11.late_ref, bf16[256,256]{1,0:T(8,128)(2,1)S(1)} %get-tuple-element.12.matrix_ref, f32[1,128]{1,0:T(1,128)S(1)} %get-tuple-element.13.sums_ref), custom_call_target="tpu_custom_call" | custom-call | tf_op jit(solution)/shard_map/rotate/pallas_call | solution.py:596

commit v4 on v3

--- a/solution.py
+++ b/solution.py
@@ -30,7 +30,8 @@
 BESIDE = {2: (1, 0), 3: (-1, 0)}
 UNITS[0] = [u_ for u_ in UNITS[0] if u_ not in BESIDE.values()] + [None, None]
 CHIPS = sorted(((jx, jy) for jx in range(4) for jy in range(4) if jx or jy), key=lambda j: (min(j[0], 4 - j[0]) + min(j[1], 4 - j[1]), j))
-OTHERS = [(jx, jy, jc) for jx, jy in CHIPS for jc in range(2)]
+HOPS = lambda j: min(j[0], 4 - j[0]) + min(j[1], 4 - j[1])
+OTHERS = sorted(((jx, jy, jc) for jx, jy in CHIPS for jc in range(2)), key=lambda j: (HOPS(j), j[2], j))
 BETAS = [7, 1, 6, 2, 5, 3, 4, 0]
 FORWARDS = [
     [(*UNITS[b_][u_], b_) for b_ in BETAS if UNITS[b_][u_] and UNITS[b_][u_][0] != 0] + ([(*BESIDE[u_], 0)] if u_ in BESIDE else [])
@@ -126,7 +127,8 @@
     def greet(h, p, j):
         pl.semaphore_signal(barrier, inc=1, device_id=(h, 2 * z + p), device_id_type=MESH)
 
-    others(greet)
+    for j, (jx, jy, jc) in reversed(list(enumerate(OTHERS))):
+        greet(up[jy][0] + ahead[jx] + cores[jc], up[jy][1], j)
     greet(partner, ylo, 0)
     smalls = [
         pltpu.make_async_copy(ref, dst, small_sem.at[i])
@@ -146,12 +148,6 @@
         for load in pair:
             load.wait()
         pack(own, packed.at[0], tmp, i)
-    for i in range(4):
-        rows = pl.ds(128 * i, 128)
-        for j in range(4):
-            there = pl.ds(128 * j, 128)
-            turned[0, there, rows] = own[0, rows, there].T
-            turned[1, there, rows] = -own[1, rows, there].T
 
     pl.semaphore_wait(barrier, 45)
 
@@ -228,6 +224,12 @@
 
     send_unit(0)
     straight(0)
+    for i in range(4):
+        rows = pl.ds(128 * i, 128)
+        for j in range(4):
+            there = pl.ds(128 * j, 128)
+            turned[0, there, rows] = own[0, rows, there].T
+            turned[1, there, rows] = -own[1, rows, there].T
     for i in range(4):
         pack(turned, packed.at[1], tmp, i)
     straight(1)

time: 51.1 us -> 50.6 us (level)
  no operation moved by 1% of the time
where the time goes in v4:
time: 50.6 us; the launch traced here: 50.5 us
  Pallas kernels  49.7 us (98%)
  between operations  0.8 us (2%)
    pallas_call x1, Pallas kernels, exchange_call(): pl.pallas_call(exchange_kernel, name='exchange', out_shape=(jax.ShapeDtyp...  47.2 us
    pallas_call x1, Pallas kernels, rotate_call(): pl.pallas_call(rotate_kernel, name='rotate', out_shape=(jax.ShapeDtypeStr...  2.51 us

profile of v4, /device:TPU:1, one launch (start us, length us, event | category | flops | bytes accessed | tf_op | source)
XLA Modules:
  0.0 50.5 jit_solution(5394130205344381348)
XLA Ops:
  0.6 47.2 %exchange.1 = (f32[4,256,512]{2,1,0:T(8,128)S(1)}, f32[4,16,2,8,128]{4,3,2,1,0:T(8,128)S(1)}, bf16[256,256]{1,0:T(8,128)(2,1)S(1)}, f32[1,128]{1,0:T(1,128)S(1)}) custom-call(f32[512,512]{1,0:T(8,128)} %re_hbm.1, f32[512,512]{1,0:T(8,128)} %im_hbm.1, f32[16,16]{1,0:T(8,128)} %ure_hbm.1, f32[16,16]{1,0:T(8,128)} %uim_hbm.1, f32[3,8]{1,0:T(4,128)} %bitcast.2, ...), custom_call_target="tpu_custom_call" | custom-call | tf_op jit(solution)/shard_map/exchange/pallas_call | solution.py:374
  47.8 2.5 %rotate.1 = (f32[512,512]{1,0:T(8,128)}, f32[512,512]{1,0:T(8,128)}, f32[1,1]{1,0:T(1,128)}) custom-call(f32[4,256,512]{2,1,0:T(8,128)S(1)} %get-tuple-element.10.early_ref, f32[4,16,2,8,128]{4,3,2,1,0:T(8,128)S(1)} %get-tuple-element.11.late_ref, bf16[256,256]{1,0:T(8,128)(2,1)S(1)} %get-tuple-element.12.matrix_ref, f32[1,128]{1,0:T(1,128)S(1)} %get-tuple-element.13.sums_ref), custom_call_target="tpu_custom_call" | custom-call | tf_op jit(solution)/shard_map/rotate/pallas_call | solution.py:598

commit v5 on v4

--- a/solution.py
+++ b/solution.py
@@ -82,6 +82,20 @@
         for m in range(2):
             at = 16 * h + 4 * q + 2 * m
             dst[at, part], dst[at + 1, part] = halve(tmp[n, 2 * m], tmp[n, 2 * m + 1], even, 32)
+
+
+def unpack(ref, tmp, rows):
+    low = lanes() < 64
+    even = (lanes() // 32) % 2 == 0
+    groups = [(g, part, q) for g in rows for part in range(2) for q in range(4)]
+    for n, (g, part, q) in enumerate(groups):
+        for m in range(2):
+            tmp[n, m], tmp[n, m + 2] = halve(ref[g, 4 * q + m, part], ref[g, 4 * q + m + 2, part], low, 64)
+    for n, (g, part, q) in enumerate(groups):
+        for m in range(2):
+            a, b = tmp[n, 2 * m], tmp[n, 2 * m + 1]
+            ref[g, 4 * q + 2 * m, part] = jnp.where(even, a, pltpu.roll(b, 32, 1))
+            ref[g, 4 * q + 2 * m + 1, part] = jnp.where(even, pltpu.roll(a, 96, 1), b)
 
 
 def exchange_kernel(
@@ -351,6 +365,8 @@
     on_lanes(f_ref, right1, 2, 14, 14, 2)
     for g in (0, 4, 6, 8, 10, 12):
         over_g2(g, turned2.at[pl.ds(g, 2)])
+    for rows in ((0, 1, 4, 5), (6, 7, 8, 9), (10, 11, 12, 13)):
+        unpack(turned2, tmp, rows)
     for n in range(8):
         v = jnp.concatenate([turned2[:, 2 * n + m].reshape(256, 128) for m in range(2)], axis=1)
         early_ref[n // 2, :, 256 * (n % 2) : 256 * (n % 2) + 256] = dot3((left[0], left[1]), halves(v))
@@ -364,6 +380,7 @@
     on_lanes(f_ref, right1, 14, 2, 4, 10)
     over_g2(2, late_ref.at[pl.ds(0, 2)])
     over_g2(14, late_ref.at[pl.ds(2, 2)])
+    unpack(late_ref, tmp, range(4))
 
 
 def exchange_call(*args):
@@ -530,7 +547,7 @@
     store_halves(right2, jnp.where(i % 8 == j % 8, value, 0.0))
     on_s = one_hot(256, 8, by_row(8) % 8)
     low = [spread(on_s, m, on_s) for m in low]
-    real = lambda value: jnp.where(same, value[0], jnp.where(lower, value[1], -value[1]))
+    real = lambda value: KEEP * jnp.where(same, value[0], jnp.where(lower, value[1], -value[1]))
     store_halves(left, real(times(u, low)))
     n = (by_row(16) // 16) % 4
     in_g = one_hot(256, 16, (n + jnp.where(n < 2, 2, 12) + 2 * z) % 16)
@@ -548,7 +565,7 @@
         f_ref[(*here, part)] = v[:, 128 * part : 128 * part + 128].reshape(n, n2, 8, 128)
 
 
-def rotate_kernel(early_ref, late_ref, matrix_ref, sums_ref, re_ref, im_ref, purity_ref, stage, rotated, tmp, sem):
+def rotate_kernel(early_ref, late_ref, matrix_ref, sums_ref, re_ref, im_ref, purity_ref, purity, stage, product, sem, purity_sem):
     r, c = lax.axis_index("row"), lax.axis_index("col")
     sums = sums_ref[...]
     lane = lanes((1, 128))
@@ -556,32 +573,21 @@
     dim = GATE * GATE * LOW
     shifts = (jnp.where(r == c, MIX * trace_re / dim, 0.0), jnp.where(r == c, MIX * trace_im / dim, 0.0))
     squared = trace_re * trace_re + trace_im * trace_im
-    purity_ref[0, 0] = (KEEP * KEEP * total + (2 * KEEP * MIX + MIX * MIX) * squared / dim) / (dim * dim)
+    purity[0, 0] = (KEEP * KEEP * total + (2 * KEEP * MIX + MIX * MIX) * squared / dim) / (dim * dim)
     matrix = matrix_ref[...]
     sublane = lax.broadcasted_iota(jnp.int32, (8, 128), 0)
-    low = lanes() < 64
-    even = (lanes() // 32) % 2 == 0
-    copies = []
-
-    def product(q):
-        v = jnp.concatenate([late_ref[:, 4 * q + m].reshape(64, 128) for m in range(4)], axis=1)
-        hi, lo = halves(v)
-        rotated[q] = early_ref[q] + dot(matrix, jnp.concatenate([hi, hi, lo, jnp.zeros_like(hi)], axis=0))
-
-    product(0)
+    v = jnp.concatenate([late_ref[:, n].reshape(64, 128) for n in range(16)], axis=1)
+    hi, lo = halves(v)
+    product[...] = dot(matrix, jnp.concatenate([hi, hi, lo, jnp.zeros_like(hi)], axis=0))
+    copies = [pltpu.make_async_copy(purity, purity_ref, purity_sem)]
+    copies[0].start()
     for q in range(4):
-        if q < 3:
-            product(q + 1)
-        for n in range(32):
-            tiles = [rotated[q, 8 * n : 8 * n + 8, 128 * m : 128 * m + 128] for m in range(4)]
-            for m in range(2):
-                tmp[q, n, m], tmp[q, n, m + 2] = halve(tiles[m], tiles[m + 2], low, 64)
-        for n in range(32):
-            g, part = n // 2, n % 2
-            for m in range(2):
-                a, b = KEEP * tmp[q, n, 2 * m], KEEP * tmp[q, n, 2 * m + 1]
-                pair = (jnp.where(even, a, pltpu.roll(b, 32, 1)), jnp.where(even, pltpu.roll(a, 96, 1), b))
-                for k, tile in zip((2 * m, 2 * m + 1), pair):
+        for g in range(16):
+            for part in range(2):
+                for k in range(4):
+                    row, col = 16 * g + 8 * part, 128 * k
+                    tile = early_ref[q, row : row + 8, col : col + 128]
+                    tile = tile + product[row : row + 8, 512 * q + col : 512 * q + col + 128]
                     if g // 4 == q:
                         tile = tile + jnp.where(lanes() == sublane + (32 * (g % 4) + 8 * k), shifts[part], 0.0)
                     stage[part, q, 32 * g + 8 * k : 32 * g + 8 * k + 8] = tile
@@ -604,12 +610,13 @@
             jax.ShapeDtypeStruct((1, 1), f32),
         ),
         in_specs=[vmem] * 4,
-        out_specs=(hbm, hbm, pl.BlockSpec(memory_space=pltpu.SMEM)),
+        out_specs=(hbm, hbm, hbm),
         scratch_shapes=[
+            pltpu.SMEM((1, 1), f32),
             pltpu.VMEM((2, 4, 512, 128), f32),
-            pltpu.VMEM((4, 256, 512), f32),
-            pltpu.VMEM((4, 32, 4, 8, 128), f32),
+            pltpu.VMEM((256, 2048), f32),
             pltpu.SemaphoreType.DMA((2, 4)),
+            pltpu.SemaphoreType.DMA,
         ],
         compiler_params=pltpu.CompilerParams(vmem_limit_bytes=20 * 2**20),
     )(*args)

time: 50.6 us -> 50 us (0.988)
  Pallas kernels: 49.7 us -> 49.1 us
    pallas_call x1, Pallas kernels: 2.51 us -> 1.63 us  [rotate_call(): pl.pallas_call(rotate_kernel, name='rotate', out_shape=(jax.ShapeDtypeStr...]
where the time goes in v5:
time: 50 us; the launch traced here: 49.9 us
  Pallas kernels  49.1 us (98%)
  between operations  0.8 us (2%)
    pallas_call x1, Pallas kernels, exchange_call(): pl.pallas_call(exchange_kernel, name='exchange', out_shape=(jax.ShapeDtyp...  47.5 us
    pallas_call x1, Pallas kernels, rotate_call(): pl.pallas_call(rotate_kernel, name='rotate', out_shape=(jax.ShapeDtypeStr...  1.63 us

profile of v5, /device:TPU:1, one launch (start us, length us, event | category | flops | bytes accessed | tf_op | source)
XLA Modules:
  0.0 49.9 jit_solution(13598693481230401275)
XLA Ops:
  0.6 47.5 %exchange.1 = (f32[4,256,512]{2,1,0:T(8,128)S(1)}, f32[4,16,2,8,128]{4,3,2,1,0:T(8,128)S(1)}, bf16[256,256]{1,0:T(8,128)(2,1)S(1)}, f32[1,128]{1,0:T(1,128)S(1)}) custom-call(f32[512,512]{1,0:T(8,128)} %re_hbm.1, f32[512,512]{1,0:T(8,128)} %im_hbm.1, f32[16,16]{1,0:T(8,128)} %ure_hbm.1, f32[16,16]{1,0:T(8,128)} %uim_hbm.1, f32[3,8]{1,0:T(4,128)} %bitcast.2, ...), custom_call_target="tpu_custom_call" | custom-call | tf_op jit(solution)/shard_map/exchange/pallas_call | solution.py:391
  48.1 1.6 %rotate.1 = (f32[512,512]{1,0:T(8,128)}, f32[512,512]{1,0:T(8,128)}, f32[1,1]{1,0:T(1,128)}) custom-call(f32[4,256,512]{2,1,0:T(8,128)S(1)} %get-tuple-element.10.early_ref, f32[4,16,2,8,128]{4,3,2,1,0:T(8,128)S(1)} %get-tuple-element.11.late_ref, bf16[256,256]{1,0:T(8,128)(2,1)S(1)} %get-tuple-element.12.matrix_ref, f32[1,128]{1,0:T(1,128)S(1)} %get-tuple-element.13.sums_ref), custom_call_target="tpu_custom_call" | custom-call | tf_op jit(solution)/shard_map/rotate/pallas_call | solution.py:604

commit v6 on v5

--- a/solution.py
+++ b/solution.py
@@ -131,19 +131,31 @@
         for i in range(4)
     ]
     barrier = pltpu.get_barrier_semaphore()
-    for k in (4, 3, 5, 2, 6, 1, 7):
-        for h in (r, partner):
-            pl.semaphore_signal(barrier, inc=1, device_id=(h, 2 * wrap(z + k, 8) + ylo), device_id_type=MESH)
+
+    def greet_plane(first, last):
+        for j, (jx, jy, jc) in reversed(list(enumerate(OTHERS))):
+            if first <= HOPS((jx, jy)) <= last:
+                pl.semaphore_signal(
+                    barrier, inc=1, device_id=(up[jy][0] + ahead[jx] + cores[jc], 2 * z + up[jy][1]), device_id_type=MESH
+                )
+
+    def greet_line(*steps):
+        for k in steps:
+            for h in (r, partner):
+                pl.semaphore_signal(barrier, inc=1, device_id=(h, 2 * wrap(z + k, 8) + ylo), device_id_type=MESH)
+
     for pair in loads:
         for load in pair:
             load.start()
-
-    def greet(h, p, j):
-        pl.semaphore_signal(barrier, inc=1, device_id=(h, 2 * z + p), device_id_type=MESH)
-
-    for j, (jx, jy, jc) in reversed(list(enumerate(OTHERS))):
-        greet(up[jy][0] + ahead[jx] + cores[jc], up[jy][1], j)
-    greet(partner, ylo, 0)
+    greet_plane(4, 4)
+    greet_line(4)
+    greet_plane(3, 3)
+    greet_line(3, 5)
+    greet_plane(2, 2)
+    greet_line(2, 6)
+    greet_plane(1, 1)
+    greet_line(1, 7)
+    pl.semaphore_signal(barrier, inc=1, device_id=(partner, 2 * z + ylo), device_id_type=MESH)
     smalls = [
         pltpu.make_async_copy(ref, dst, small_sem.at[i])
         for i, (ref, dst) in enumerate(

time: 50 us -> 49.9 us (level)
  no operation moved by 1% of the time
where the time goes in v6:
time: 49.9 us; the launch traced here: 49.8 us
  Pallas kernels  49 us (98%)
  between operations  0.8 us (2%)
    pallas_call x1, Pallas kernels, exchange_call(): pl.pallas_call(exchange_kernel, name='exchange', out_shape=(jax.ShapeDtyp...  47.3 us
    pallas_call x1, Pallas kernels, rotate_call(): pl.pallas_call(rotate_kernel, name='rotate', out_shape=(jax.ShapeDtypeStr...  1.63 us

profile of v6, /device:TPU:1, one launch (start us, length us, event | category | flops | bytes accessed | tf_op | source)
XLA Modules:
  0.0 49.8 jit_solution(7263819000884109184)
XLA Ops:
  0.6 47.3 %exchange.1 = (f32[4,256,512]{2,1,0:T(8,128)S(1)}, f32[4,16,2,8,128]{4,3,2,1,0:T(8,128)S(1)}, bf16[256,256]{1,0:T(8,128)(2,1)S(1)}, f32[1,128]{1,0:T(1,128)S(1)}) custom-call(f32[512,512]{1,0:T(8,128)} %re_hbm.1, f32[512,512]{1,0:T(8,128)} %im_hbm.1, f32[16,16]{1,0:T(8,128)} %ure_hbm.1, f32[16,16]{1,0:T(8,128)} %uim_hbm.1, f32[3,8]{1,0:T(4,128)} %bitcast.2, ...), custom_call_target="tpu_custom_call" | custom-call | tf_op jit(solution)/shard_map/exchange/pallas_call | solution.py:403
  48.0 1.6 %rotate.1 = (f32[512,512]{1,0:T(8,128)}, f32[512,512]{1,0:T(8,128)}, f32[1,1]{1,0:T(1,128)}) custom-call(f32[4,256,512]{2,1,0:T(8,128)S(1)} %get-tuple-element.10.early_ref, f32[4,16,2,8,128]{4,3,2,1,0:T(8,128)S(1)} %get-tuple-element.11.late_ref, bf16[256,256]{1,0:T(8,128)(2,1)S(1)} %get-tuple-element.12.matrix_ref, f32[1,128]{1,0:T(1,128)S(1)} %get-tuple-element.13.sums_ref), custom_call_target="tpu_custom_call" | custom-call | tf_op jit(solution)/shard_map/rotate/pallas_call | solution.py:616

commit v7 on v6

--- a/solution.py
+++ b/solution.py
@@ -118,7 +118,7 @@
 
     def others(fn):
         for j, (jx, jy, jc) in enumerate(OTHERS):
-            fn(up[jy][0] + ahead[jx] + cores[jc], up[jy][1], j)
+            fn(up[jy][0] + ahead[jx] + 1 - jc, up[jy][1], jnp.where(core == 1, OTHERS.index((jx, jy, 0)), OTHERS.index((jx, jy, 1))))
 
     def copy(src, dst, send, recv, row, col):
         return pltpu.make_async_remote_copy(src, dst, send, recv, device_id=(row, col), device_id_type=MESH)
@@ -301,13 +301,13 @@
 
     def pass_on():
         for j, (jx, jy, jc) in enumerate(OTHERS):
-            if j == 8:
+            if j == 4:
                 send_unit(1)
             bs = wrap(wrap(down[jy][0] + behind[jx] + 8 - z, 8), 8)
             dz = pick(bs, [UNITS[b][0][0] % 8 for b in range(8)])
             a, b = wrap(8 - dz, 8), wrap(bs + 8 - dz, 8)
             copy(mu.at[j], mu.at[j], s1, ru.at[j], r, c).wait_recv()
-            dst = f_ref.at[2 * b + cores[jc], 2 * a + down[jy][1]]
+            dst = f_ref.at[2 * b + 1 - jc, 2 * a + down[jy][1]]
             copy(mu.at[j], dst, s2, r2.at[0], r, 2 * wrap(z + dz, 8) + ylo).start()
 
     def forward(u):

time: 49.9 us -> 49.8 us (level)
  no operation moved by 1% of the time
where the time goes in v7:
time: 49.8 us; the launch traced here: 49.7 us
  Pallas kernels  48.9 us (98%)
  between operations  0.8 us (2%)
    pallas_call x1, Pallas kernels, exchange_call(): pl.pallas_call(exchange_kernel, name='exchange', out_shape=(jax.ShapeDtyp...  47.2 us
    pallas_call x1, Pallas kernels, rotate_call(): pl.pallas_call(rotate_kernel, name='rotate', out_shape=(jax.ShapeDtypeStr...  1.63 us

profile of v7, /device:TPU:1, one launch (start us, length us, event | category | flops | bytes accessed | tf_op | source)
XLA Modules:
  0.0 49.7 jit_solution(14210946310883369075)
XLA Ops:
  0.6 47.2 %exchange.1 = (f32[4,256,512]{2,1,0:T(8,128)S(1)}, f32[4,16,2,8,128]{4,3,2,1,0:T(8,128)S(1)}, bf16[256,256]{1,0:T(8,128)(2,1)S(1)}, f32[1,128]{1,0:T(1,128)S(1)}) custom-call(f32[512,512]{1,0:T(8,128)} %re_hbm.1, f32[512,512]{1,0:T(8,128)} %im_hbm.1, f32[16,16]{1,0:T(8,128)} %ure_hbm.1, f32[16,16]{1,0:T(8,128)} %uim_hbm.1, f32[3,8]{1,0:T(4,128)} %bitcast.2, ...), custom_call_target="tpu_custom_call" | custom-call | tf_op jit(solution)/shard_map/exchange/pallas_call | solution.py:403
  47.9 1.6 %rotate.1 = (f32[512,512]{1,0:T(8,128)}, f32[512,512]{1,0:T(8,128)}, f32[1,1]{1,0:T(1,128)}) custom-call(f32[4,256,512]{2,1,0:T(8,128)S(1)} %get-tuple-element.10.early_ref, f32[4,16,2,8,128]{4,3,2,1,0:T(8,128)S(1)} %get-tuple-element.11.late_ref, bf16[256,256]{1,0:T(8,128)(2,1)S(1)} %get-tuple-element.12.matrix_ref, f32[1,128]{1,0:T(1,128)S(1)} %get-tuple-element.13.sums_ref), custom_call_target="tpu_custom_call" | custom-call | tf_op jit(solution)/shard_map/rotate/pallas_call | solution.py:616

commit v8 on v7

--- a/solution.py
+++ b/solution.py
@@ -301,7 +301,7 @@
 
     def pass_on():
         for j, (jx, jy, jc) in enumerate(OTHERS):
-            if j == 4:
+            if j == 8:
                 send_unit(1)
             bs = wrap(wrap(down[jy][0] + behind[jx] + 8 - z, 8), 8)
             dz = pick(bs, [UNITS[b][0][0] % 8 for b in range(8)])

time: 49.8 us -> 49.8 us (level)
  no operation moved by 1% of the time
where the time goes in v8:
time: 49.8 us; the launch traced here: 49.7 us
  Pallas kernels  48.9 us (98%)
  between operations  0.8 us (2%)
    pallas_call x1, Pallas kernels, exchange_call(): pl.pallas_call(exchange_kernel, name='exchange', out_shape=(jax.ShapeDtyp...  47.2 us
    pallas_call x1, Pallas kernels, rotate_call(): pl.pallas_call(rotate_kernel, name='rotate', out_shape=(jax.ShapeDtypeStr...  1.63 us

profile of v8, /device:TPU:1, one launch (start us, length us, event | category | flops | bytes accessed | tf_op | source)
XLA Modules:
  0.0 49.7 jit_solution(11468918003517770706)
XLA Ops:
  0.6 47.2 %exchange.1 = (f32[4,256,512]{2,1,0:T(8,128)S(1)}, f32[4,16,2,8,128]{4,3,2,1,0:T(8,128)S(1)}, bf16[256,256]{1,0:T(8,128)(2,1)S(1)}, f32[1,128]{1,0:T(1,128)S(1)}) custom-call(f32[512,512]{1,0:T(8,128)} %re_hbm.1, f32[512,512]{1,0:T(8,128)} %im_hbm.1, f32[16,16]{1,0:T(8,128)} %ure_hbm.1, f32[16,16]{1,0:T(8,128)} %uim_hbm.1, f32[3,8]{1,0:T(4,128)} %bitcast.2, ...), custom_call_target="tpu_custom_call" | custom-call | tf_op jit(solution)/shard_map/exchange/pallas_call | solution.py:403
  47.9 1.6 %rotate.1 = (f32[512,512]{1,0:T(8,128)}, f32[512,512]{1,0:T(8,128)}, f32[1,1]{1,0:T(1,128)}) custom-call(f32[4,256,512]{2,1,0:T(8,128)S(1)} %get-tuple-element.10.early_ref, f32[4,16,2,8,128]{4,3,2,1,0:T(8,128)S(1)} %get-tuple-element.11.late_ref, bf16[256,256]{1,0:T(8,128)(2,1)S(1)} %get-tuple-element.12.matrix_ref, f32[1,128]{1,0:T(1,128)S(1)} %get-tuple-element.13.sums_ref), custom_call_target="tpu_custom_call" | custom-call | tf_op jit(solution)/shard_map/rotate/pallas_call | solution.py:616

commit v9 on v8

--- a/solution.py
+++ b/solution.py
@@ -38,7 +38,7 @@
     for u_ in range(8)
 ]
 SLOT = {f_: i_ for i_, f_ in enumerate(f_ for fs_ in FORWARDS[1:] for f_ in fs_)}
-AHEAD = {1:[2,3],2:[4],3:[5,6],4:[7],5:[]}
+AHEAD = {1:[2,3],2:[4,5],3:[6],4:[7],5:[]}
 
 
 def group(dz, kind):

time: 49.8 us -> 49.8 us (level)
  no operation moved by 1% of the time
where the time goes in v9:
time: 49.8 us; the launch traced here: 49.7 us
  Pallas kernels  48.9 us (98%)
  between operations  0.8 us (2%)
    pallas_call x1, Pallas kernels, exchange_call(): pl.pallas_call(exchange_kernel, name='exchange', out_shape=(jax.ShapeDtyp...  47.2 us
    pallas_call x1, Pallas kernels, rotate_call(): pl.pallas_call(rotate_kernel, name='rotate', out_shape=(jax.ShapeDtypeStr...  1.63 us

profile of v9, /device:TPU:1, one launch (start us, length us, event | category | flops | bytes accessed | tf_op | source)
XLA Modules:
  0.0 49.7 jit_solution(6602317536971572990)
XLA Ops:
  0.6 47.2 %exchange.1 = (f32[4,256,512]{2,1,0:T(8,128)S(1)}, f32[4,16,2,8,128]{4,3,2,1,0:T(8,128)S(1)}, bf16[256,256]{1,0:T(8,128)(2,1)S(1)}, f32[1,128]{1,0:T(1,128)S(1)}) custom-call(f32[512,512]{1,0:T(8,128)} %re_hbm.1, f32[512,512]{1,0:T(8,128)} %im_hbm.1, f32[16,16]{1,0:T(8,128)} %ure_hbm.1, f32[16,16]{1,0:T(8,128)} %uim_hbm.1, f32[3,8]{1,0:T(4,128)} %bitcast.2, ...), custom_call_target="tpu_custom_call" | custom-call | tf_op jit(solution)/shard_map/exchange/pallas_call | solution.py:403
  47.9 1.6 %rotate.1 = (f32[512,512]{1,0:T(8,128)}, f32[512,512]{1,0:T(8,128)}, f32[1,1]{1,0:T(1,128)}) custom-call(f32[4,256,512]{2,1,0:T(8,128)S(1)} %get-tuple-element.10.early_ref, f32[4,16,2,8,128]{4,3,2,1,0:T(8,128)S(1)} %get-tuple-element.11.late_ref, bf16[256,256]{1,0:T(8,128)(2,1)S(1)} %get-tuple-element.12.matrix_ref, f32[1,128]{1,0:T(1,128)S(1)} %get-tuple-element.13.sums_ref), custom_call_target="tpu_custom_call" | custom-call | tf_op jit(solution)/shard_map/rotate/pallas_call | solution.py:616

commit v10 on v8

--- a/solution.py
+++ b/solution.py
@@ -301,7 +301,7 @@
 
     def pass_on():
         for j, (jx, jy, jc) in enumerate(OTHERS):
-            if j == 8:
+            if j == 6:
                 send_unit(1)
             bs = wrap(wrap(down[jy][0] + behind[jx] + 8 - z, 8), 8)
             dz = pick(bs, [UNITS[b][0][0] % 8 for b in range(8)])

time: 49.8 us -> 49.8 us (level)
  no operation moved by 1% of the time
where the time goes in v10:
time: 49.8 us; the launch traced here: 49.7 us
  Pallas kernels  48.9 us (98%)
  between operations  0.8 us (2%)
    pallas_call x1, Pallas kernels, exchange_call(): pl.pallas_call(exchange_kernel, name='exchange', out_shape=(jax.ShapeDtyp...  47.2 us
    pallas_call x1, Pallas kernels, rotate_call(): pl.pallas_call(rotate_kernel, name='rotate', out_shape=(jax.ShapeDtypeStr...  1.63 us

profile of v10, /device:TPU:1, one launch (start us, length us, event | category | flops | bytes accessed | tf_op | source)
XLA Modules:
  0.0 49.7 jit_solution(15513221869966865388)
XLA Ops:
  0.6 47.2 %exchange.1 = (f32[4,256,512]{2,1,0:T(8,128)S(1)}, f32[4,16,2,8,128]{4,3,2,1,0:T(8,128)S(1)}, bf16[256,256]{1,0:T(8,128)(2,1)S(1)}, f32[1,128]{1,0:T(1,128)S(1)}) custom-call(f32[512,512]{1,0:T(8,128)} %re_hbm.1, f32[512,512]{1,0:T(8,128)} %im_hbm.1, f32[16,16]{1,0:T(8,128)} %ure_hbm.1, f32[16,16]{1,0:T(8,128)} %uim_hbm.1, f32[3,8]{1,0:T(4,128)} %bitcast.2, ...), custom_call_target="tpu_custom_call" | custom-call | tf_op jit(solution)/shard_map/exchange/pallas_call | solution.py:403
  47.9 1.6 %rotate.1 = (f32[512,512]{1,0:T(8,128)}, f32[512,512]{1,0:T(8,128)}, f32[1,1]{1,0:T(1,128)}) custom-call(f32[4,256,512]{2,1,0:T(8,128)S(1)} %get-tuple-element.10.early_ref, f32[4,16,2,8,128]{4,3,2,1,0:T(8,128)S(1)} %get-tuple-element.11.late_ref, bf16[256,256]{1,0:T(8,128)(2,1)S(1)} %get-tuple-element.12.matrix_ref, f32[1,128]{1,0:T(1,128)S(1)} %get-tuple-element.13.sums_ref), custom_call_target="tpu_custom_call" | custom-call | tf_op jit(solution)/shard_map/rotate/pallas_call | solution.py:616
